TPU v7x, 32 devices: a whole 2x2x4 slice. The times are simulated.
32 devices in a mesh: cand: 2 (over y), gx: 8 (over z, x), gy: 2 (over core).
Axes of the slice: x: 2, y: 2, z: 4, core: 2. Of those that a mesh axis runs over, the one named last changes fastest.
Arguments:
- electric: float32 [2, 3, 64, 64, 128], P(None, None, ('cand', 'gx'), 'gy'), parts along dimension 2, may hold values from -6 to 6
- magnetic: float32 [2, 3, 64, 64, 128], P(None, None, ('cand', 'gx'), 'gy'), parts along dimension 2, may hold values from -6 to 6
- density: float32 [64, 64, 128], P(('cand', 'gx'), 'gy'), parts along dimension 0, may hold values from 0 to 0.1
- design_mask: int32 [64, 64, 128], P(('cand', 'gx'), 'gy'), parts along dimension 0, may hold values 0 or 1
- planes: int32 [4], P('cand'), parts along dimension 0, may hold values from 8 to 119
- profiles: float32 [2, 64, 64], P(None, ('cand', 'gx'), 'gy'), parts along dimension 1, may hold values from -6 to 6
- waveforms: float32 [2, 16], P(None, 'cand'), parts along dimension 1, may hold values from -4 to 4
Outputs:
- electric_out: float32 [2, 3, 64, 64, 128], P(None, None, ('cand', 'gx'), 'gy'), parts along dimension 2
- magnetic_out: float32 [2, 3, 64, 64, 128], P(None, None, ('cand', 'gx'), 'gy'), parts along dimension 2
- gradient: float32 [64, 64, 128], P(('cand', 'gx'), 'gy'), parts along dimension 0
There are 2 independent parts, one for each index of `cand`. A program takes and returns all parts, laid end to end along the dimension named above; each array names one. Nothing has to cross between parts.
All inputs are finite; a program needn't handle non-finite values. No bound on the sum of `design_mask` on one device may be relied on, other than what follows from the above.
Results may differ from a plain program's by a relative error of at most 0.00016.
Values sent between devices are 32-bit elements; how exact they have to be, the bound alone decides.
A program may use at most 64 MiB of HBM per device.

v0:
```python
import jax
import jax.numpy as jnp
from jax import lax
from jax.sharding import PartitionSpec as P

STEPS = 8
PMLW = 8


step_dt = 0.7
contrast = 5.0
sigma_max = 2.0
small_eps = 1e-06
inv_spacing = 0.5


def with_halo(block, sides, width):
    for axis, dim in sides:
        count = lax.axis_size(axis)
        forward = [(i, i + 1) for i in range(count - 1)]
        backward = [(target, source) for source, target in forward]
        low = lax.ppermute(
            lax.slice_in_dim(block, block.shape[dim] - width, None, axis=dim), axis, forward
        )
        high = lax.ppermute(lax.slice_in_dim(block, 0, width, axis=dim), axis, backward)
        block = jnp.concatenate([low, block, high], axis=dim)
    return block


def coefficients(depth_cells, layer):
    zpos = jnp.arange(depth_cells).astype(jnp.float32)
    lower = (layer - zpos - 0.5) / layer
    upper = (zpos + 0.5 - (depth_cells - layer)) / layer
    depth = jnp.maximum(jnp.maximum(lower, upper), 0.0)
    sigma = sigma_max * depth * depth * depth
    half = sigma * step_dt / 2.0
    return ((1.0 - half) / (1.0 + half), step_dt / (1.0 + half))


def fwd_diff(field, upper, axis):
    rest = lax.slice_in_dim(field, 1, field.shape[axis], axis=axis)
    return jnp.concatenate([rest, upper], axis) - field


def bwd_diff(field, lower, axis):
    rest = lax.slice_in_dim(field, 0, field.shape[axis] - 1, axis=axis)
    return field - jnp.concatenate([lower, rest], axis)


def fwd_z(field):
    return (
        jnp.concatenate([field[..., 1:], jnp.zeros_like(field[..., :1])], -1) - field
    ) * inv_spacing


def bwd_z(field):
    return (
        field - jnp.concatenate([jnp.zeros_like(field[..., :1]), field[..., :-1]], -1)
    ) * inv_spacing


def magnetic_update(elec, magn, x_upper, y_upper, decay, gain):
    ex, ey, ez = (elec[:, 0], elec[:, 1], elec[:, 2])
    curl_x = fwd_diff(ez, y_upper[:, 1], 2) * inv_spacing - fwd_z(ey)
    curl_y = fwd_z(ex) - fwd_diff(ez, x_upper[:, 1], 1)
    curl_z = fwd_diff(ey, x_upper[:, 0], 1) - fwd_diff(ex, y_upper[:, 0], 2) * inv_spacing
    curl = jnp.stack([curl_x, curl_y, curl_z], 1)
    return decay * magn - gain * curl


def electric_update(elec, magn, x_lower, y_lower, decay, gain, inv_eps, drive):
    hx, hy, hz = (magn[:, 0], magn[:, 1], magn[:, 2])
    curl_x = bwd_diff(hz, y_lower[:, 1], 2) * inv_spacing - bwd_z(hy)
    curl_y = bwd_z(hx) - bwd_diff(hz, x_lower[:, 1], 1)
    curl_z = bwd_diff(hy, x_lower[:, 0], 1) - bwd_diff(hx, y_lower[:, 0], 2) * inv_spacing
    new_x = decay * elec[:, 0] + gain * (inv_eps * curl_x - drive)
    new_y = decay * elec[:, 1] + gain * (inv_eps * curl_y)
    new_z = decay * elec[:, 2] + gain * (inv_eps * curl_z)
    return jnp.stack([new_x, new_y, new_z], 1)


def correlate(elec):
    return jnp.sum(elec[0] * elec[1], axis=0)


def inside_mask(count, start, total):
    where = start + jnp.arange(count)
    return ((where >= 0) & (where < total)).astype(jnp.float32)


def shards(electric, magnetic, density, design_mask, planes, profiles, waveforms):
    sets, comps, width_x, width_y, depth_z = electric.shape
    decay, gain = coefficients(depth_z, PMLW)
    flags = design_mask.astype(jnp.float32)
    inv_eps = 1.0 / (1.0 + contrast * density * flags)
    zidx = jnp.arange(depth_z)
    source = profiles[0][:, :, None] * (zidx == planes[0]).astype(jnp.float32)
    adjoint = profiles[1][:, :, None] * (zidx == planes[1]).astype(jnp.float32)
    probe = (zidx == planes[1]).astype(jnp.float32)
    total_x = width_x * lax.axis_size("gx")
    total_y = width_y * lax.axis_size("gy")
    elec, magn = (electric, magnetic)
    corr = jnp.zeros((width_x, width_y, depth_z), jnp.float32)
    rim = 2
    inv_wide, source_wide, adjoint_wide = (
        with_halo(inv_eps, (("gx", 0), ("gy", 1)), rim),
        with_halo(source, (("gx", 0), ("gy", 1)), rim),
        with_halo(adjoint, (("gx", 0), ("gy", 1)), rim),
    )
    valid_x = inside_mask(width_x + 2 * rim, lax.axis_index("gx") * width_x - rim, total_x)
    valid_y = inside_mask(width_y + 2 * rim, lax.axis_index("gy") * width_y - rim, total_y)
    valid = valid_x[:, None, None] * valid_y[None, :, None]
    x_zero = jnp.zeros((sets, 2, 1, width_y + 2 * rim, depth_z), jnp.float32)
    y_zero = jnp.zeros((sets, 2, width_x + 2 * rim, 1, depth_z), jnp.float32)
    for rounds in range(STEPS // rim):
        elec_wide, magn_wide = (
            with_halo(elec, (("gx", 2), ("gy", 3)), rim),
            with_halo(magn, (("gx", 2), ("gy", 3)), rim),
        )
        for inner_step in range(rim):
            step = rounds * rim + inner_step
            magn_wide = magnetic_update(elec_wide, magn_wide, x_zero, y_zero, decay, gain) * valid
            drive = jnp.stack([source_wide * waveforms[0, step], adjoint_wide * waveforms[1, step]])
            elec_wide = (
                electric_update(elec_wide, magn_wide, x_zero, y_zero, decay, gain, inv_wide, drive)
                * valid
            )
            corr = corr + correlate(elec_wide[:, :, rim : rim + width_x, rim : rim + width_y])
        elec = elec_wide[:, :, rim : rim + width_x, rim : rim + width_y]
        magn = magn_wide[:, :, rim : rim + width_x, rim : rim + width_y]
    local_power = jnp.sum(elec[0] * elec[0] * probe)
    power = lax.psum(local_power, ("gx", "gy")) / (total_x * total_y)
    gradient = flags * contrast * inv_eps * inv_eps * step_dt * corr / (power + small_eps)
    return (elec, magn, gradient)


def solution(mesh):
    return jax.shard_map(
        shards,
        mesh=mesh,
        in_specs=(
            P(None, None, ("cand", "gx"), "gy", None),
            P(None, None, ("cand", "gx"), "gy", None),
            P(("cand", "gx"), "gy", None),
            P(("cand", "gx"), "gy", None),
            P("cand"),
            P(None, ("cand", "gx"), "gy"),
            P(None, "cand"),
        ),
        out_specs=(
            P(None, None, ("cand", "gx"), "gy", None),
            P(None, None, ("cand", "gx"), "gy", None),
            P(("cand", "gx"), "gy", None),
        ),
        check_vma=False,
    )
```

profile of v0, /device:TPU:0, one launch (start us, length us, event | category | flops | bytes accessed | tf_op | source)
XLA Modules:
  0.0 207.4 jit_solution(15865446127598994551)
XLA Ops:
  0.6 1.0 fusion.53
  1.7 4.9 %collective-permute-start.4 = (f32[2,32,128]{2,0,1:T(2,128)S(1)}, f32[2,32,128]{2,0,1:T(2,128)S(1)}, u32[]{:S(2)}, u32[]{:S(2)}) collective-permute-start(f32[2,32,128]{2,0,1:T(2,128)S(1)} %get-tuple-element.162), channel_id=1, source_target_pairs={{0,2},{2,4},{4,6},{6,8},{8,10},{10,12},{12,14},{1,3},{3,5},{5,7},{... | collective-permute-start | bytes 98312 | tf_op jit(solution)/shard_map/ppermute | solution.py:22
  6.6 1.3 collective-permute-start.5
  7.9 1.3 fusion.71
  10.8 4.5 %collective-permute-start.16 = (f32[2,32,128]{2,0,1:T(2,128)S(1)}, f32[2,32,128]{2,0,1:T(2,128)S(1)}, u32[]{:S(2)}, u32[]{:S(2)}) collective-permute-start(f32[2,32,128]{2,0,1:T(2,128)S(1)} %get-tuple-element.160), channel_id=1, source_target_pairs={{0,2},{2,4},{4,6},{6,8},{8,10},{10,12},{12,14},{1,3},{3,5},{5,7},{... | collective-permute-start | bytes 98312 | tf_op jit(solution)/shard_map/ppermute | solution.py:22
  16.2 4.4 %collective-permute-start.12 = (f32[2,32,128]{2,0,1:T(2,128)S(1)}, f32[2,32,128]{2,0,1:T(2,128)S(1)}, u32[]{:S(2)}, u32[]{:S(2)}) collective-permute-start(f32[2,32,128]{2,0,1:T(2,128)S(1)} %get-tuple-element.158), channel_id=1, source_target_pairs={{0,2},{2,4},{4,6},{6,8},{8,10},{10,12},{12,14},{1,3},{3,5},{5,7},{... | collective-permute-start | bytes 98312 | tf_op jit(solution)/shard_map/ppermute | solution.py:22
  20.6 1.3 collective-permute-start.13
  25.0 1.3 collective-permute-start.17
  26.4 5.1 %collective-permute-start.8 = (f32[2,3,2,32,128]{4,2,3,0,1:T(2,128)S(1)}, f32[2,3,2,32,128]{4,2,3,0,1:T(2,128)S(1)}, u32[]{:S(2)}, u32[]{:S(2)}) collective-permute-start(f32[2,3,2,32,128]{4,2,3,0,1:T(2,128)S(1)} %get-tuple-element.130), channel_id=1, source_target_pairs={{0,2},{2,4},{4,6},{6,8},{8,10},{10,12},{12,14},{1,3},{3,5},{5,7},{... | collective-permute-start | bytes 589832 | tf_op jit(solution)/shard_map/ppermute | solution.py:22
  31.6 4.8 %collective-permute-start = (f32[2,3,2,32,128]{4,2,3,0,1:T(2,128)S(1)}, f32[2,3,2,32,128]{4,2,3,0,1:T(2,128)S(1)}, u32[]{:S(2)}, u32[]{:S(2)}) collective-permute-start(f32[2,3,2,32,128]{4,2,3,0,1:T(2,128)S(1)} %get-tuple-element.128), channel_id=1, source_target_pairs={{0,2},{2,4},{4,6},{6,8},{8,10},{10,12},{12,14},{1,3},{3,5},{5,7},{... | collective-permute-start | bytes 589832 | tf_op jit(solution)/shard_map/ppermute | solution.py:22
  36.4 1.3 collective-permute-start.1
  37.8 1.3 collective-permute-start.18
  39.1 1.3 collective-permute-start.19
  40.4 3.0 %collective-permute-start.14 = (f32[8,2,128]{2,0,1:T(8,128)S(1)}, f32[8,2,128]{2,0,1:T(8,128)S(1)}, u32[]{:S(2)}, u32[]{:S(2)}) collective-permute-start(f32[8,2,128]{2,0,1:T(8,128)S(1)} %get-tuple-element.148), channel_id=1, source_target_pairs={{0,1},{2,3},{4,5},{6,7},{8,9},{10,11},{12,13},{14,15},{16,17},{18,... | collective-permute-start | bytes 24584 | tf_op jit(solution)/shard_map/ppermute | solution.py:22
  43.5 1.3 collective-permute-start.15
  44.8 2.5 %broadcast_multiply_fusion = (f32[1,8,36,128]{3,1,2,0:T(8,128)S(1)}, f32[1,8,36,128]{3,1,2,0:T(8,128)S(1)}, f32[1,8,36,128]{3,1,2,0:T(8,128)S(1)}, f32[1,8,36,128]{3,1,2,0:T(8,128)S(1)}) fusion(f32[]{:T(128)} %bitcast.117, f32[1,8,2,128]{3,1,2,0:T(8,128)S(1)} %bitcast.540, f32[1,8,32,128]{3,1,2,0:T(8,128)S(1)} %get-tuple-element.154, ...), kind=kLoop, calls=%fused_computation.184 | loop fusion | flops 221184 | bytes 737296 | tf_op jit(solution)/shard_map/mul | solution.py:123
  47.3 2.4 %broadcast_multiply_fusion.2 = (f32[1,8,36,128]{3,1,2,0:T(8,128)S(1)}, f32[1,8,36,128]{3,1,2,0:T(8,128)S(1)}, f32[1,8,36,128]{3,1,2,0:T(8,128)S(1)}, f32[1,8,36,128]{3,1,2,0:T(8,128)S(1)}) fusion(f32[]{:T(128)} %bitcast.103, f32[1,8,2,128]{3,1,2,0:T(8,128)S(1)} %bitcast.541, f32[1,8,32,128]{3,1,2,0:T(8,128)S(1)} %get-tuple-element.154, ...), kind=kLoop, calls=%fused_computation.186 | loop fusion | flops 221184 | bytes 737296 | tf_op jit(solution)/shard_map/mul | solution.py:123
  49.7 3.0 %collective-permute-start.6 = (f32[8,2,128]{2,0,1:T(8,128)S(1)}, f32[8,2,128]{2,0,1:T(8,128)S(1)}, u32[]{:S(2)}, u32[]{:S(2)}) collective-permute-start(f32[8,2,128]{2,0,1:T(8,128)S(1)} %get-tuple-element.156), channel_id=1, source_target_pairs={{0,1},{2,3},{4,5},{6,7},{8,9},{10,11},{12,13},{14,15},{16,17},{18,... | collective-permute-start | bytes 24584 | tf_op jit(solution)/shard_map/ppermute | solution.py:22
  52.8 1.3 collective-permute-start.7
  54.1 2.6 %broadcast_multiply_fusion.1 = (f32[1,8,36,128]{3,1,2,0:T(8,128)S(1)}, f32[1,8,36,128]{3,1,2,0:T(8,128)S(1)}, f32[1,8,36,128]{3,1,2,0:T(8,128)S(1)}, f32[1,8,36,128]{3,1,2,0:T(8,128)S(1)}) fusion(f32[]{:T(128)} %bitcast.116, f32[1,8,2,128]{3,1,2,0:T(8,128)S(1)} %bitcast.536, f32[1,8,32,128]{3,1,2,0:T(8,128)S(1)} %get-tuple-element.150, ...), kind=kLoop, calls=%fused_computation.185 | loop fusion | flops 221184 | bytes 737296 | tf_op jit(solution)/shard_map/mul | solution.py:123
  56.7 2.5 %broadcast_multiply_fusion.3 = (f32[1,8,36,128]{3,1,2,0:T(8,128)S(1)}, f32[1,8,36,128]{3,1,2,0:T(8,128)S(1)}, f32[1,8,36,128]{3,1,2,0:T(8,128)S(1)}, f32[1,8,36,128]{3,1,2,0:T(8,128)S(1)}) fusion(f32[]{:T(128)} %bitcast.102, f32[1,8,2,128]{3,1,2,0:T(8,128)S(1)} %bitcast.537, f32[1,8,32,128]{3,1,2,0:T(8,128)S(1)} %get-tuple-element.150, ...), kind=kLoop, calls=%fused_computation.187 | loop fusion | flops 221184 | bytes 737296 | tf_op jit(solution)/shard_map/mul | solution.py:123
  59.2 1.3 collective-permute-start.9
  60.7 3.0 %collective-permute-start.2 = (f32[2,3,8,2,128]{4,2,3,0,1:T(8,128)S(1)}, f32[2,3,8,2,128]{4,2,3,0,1:T(8,128)S(1)}, u32[]{:S(2)}, u32[]{:S(2)}) collective-permute-start(f32[2,3,8,2,128]{4,2,3,0,1:T(8,128)S(1)} %get-tuple-element.124), channel_id=1, source_target_pairs={{0,1},{2,3},{4,5},{6,7},{8,9},{10,11},{12,13},{14,15},{16,17},{18,... | collective-permute-start | bytes 147464 | tf_op jit(solution)/shard_map/ppermute | solution.py:22
  63.7 1.3 collective-permute-start.3
  65.0 4.1 %collective-permute-done.9 = f32[2,3,2,32,128]{4,2,3,0,1:T(2,128)S(1)} collective-permute-done((f32[2,3,2,32,128]{4,2,3,0,1:T(2,128)S(1)}, f32[2,3,2,32,128]{4,2,3,0,1:T(2,128)S(1)}, u32[]{:S(2)}, u32[]{:S(2)}) %collective-permute-start.9) | collective-permute-done | bytes 196640 | tf_op jit(solution)/shard_map/ppermute | solution.py:25
  69.1 2.2 %collective-permute-start.10 = (f32[2,3,8,2,128]{4,2,3,0,1:T(8,128)S(1)}, f32[2,3,8,2,128]{4,2,3,0,1:T(8,128)S(1)}, u32[]{:S(2)}, u32[]{:S(2)}) collective-permute-start(f32[2,3,8,2,128]{4,2,3,0,1:T(8,128)S(1)} %get-tuple-element.126), channel_id=1, source_target_pairs={{0,1},{2,3},{4,5},{6,7},{8,9},{10,11},{12,13},{14,15},{16,17},{18,... | collective-permute-start | bytes 147464 | tf_op jit(solution)/shard_map/ppermute | solution.py:22
  71.3 1.3 collective-permute-start.11
  73.6 0.9 collective-permute-done.11
  77.5 5.0 %collective-permute-start.20 = (f32[2,3,2,32,128]{4,2,3,0,1:T(2,128)S(1)}, f32[2,3,2,32,128]{4,2,3,0,1:T(2,128)S(1)}, u32[]{:S(2)}, u32[]{:S(2)}) collective-permute-start(f32[2,3,2,32,128]{4,2,3,0,1:T(2,128)S(1)} %get-tuple-element.90), channel_id=1, source_target_pairs={{0,2},{2,4},{4,6},{6,8},{8,10},{10,12},{12,14},{1,3},{3,5},{5,7},{... | collective-permute-start | bytes 589832 | tf_op jit(solution)/shard_map/ppermute | solution.py:22
  82.5 1.3 collective-permute-start.21
  84.1 4.6 %collective-permute-start.24 = (f32[2,3,2,32,128]{4,2,3,0,1:T(2,128)S(1)}, f32[2,3,2,32,128]{4,2,3,0,1:T(2,128)S(1)}, u32[]{:S(2)}, u32[]{:S(2)}) collective-permute-start(f32[2,3,2,32,128]{4,2,3,0,1:T(2,128)S(1)} %get-tuple-element.95), channel_id=1, source_target_pairs={{0,2},{2,4},{4,6},{6,8},{8,10},{10,12},{12,14},{1,3},{3,5},{5,7},{... | collective-permute-start | bytes 589832 | tf_op jit(solution)/shard_map/ppermute | solution.py:22
  88.7 1.3 collective-permute-start.25
  90.1 1.9 collective-permute-done.20
  92.0 1.3 collective-permute-start.22
  93.3 1.3 collective-permute-start.23
  94.6 5.1 %collective-permute-done.24 = f32[2,3,2,32,128]{4,2,3,0,1:T(2,128)S(1)} collective-permute-done((f32[2,3,2,32,128]{4,2,3,0,1:T(2,128)S(1)}, f32[2,3,2,32,128]{4,2,3,0,1:T(2,128)S(1)}, u32[]{:S(2)}, u32[]{:S(2)}) %collective-permute-start.24) | collective-permute-done | bytes 196640 | tf_op jit(solution)/shard_map/ppermute | solution.py:22
  99.8 1.3 collective-permute-start.26
  101.1 1.3 collective-permute-start.27
  103.4 0.8 collective-permute-done.27
  107.4 4.4 %collective-permute-start.28 = (f32[2,3,2,32,128]{4,2,3,0,1:T(2,128)S(1)}, f32[2,3,2,32,128]{4,2,3,0,1:T(2,128)S(1)}, u32[]{:S(2)}, u32[]{:S(2)}) collective-permute-start(f32[2,3,2,32,128]{4,2,3,0,1:T(2,128)S(1)} %get-tuple-element.68), channel_id=1, source_target_pairs={{0,2},{2,4},{4,6},{6,8},{8,10},{10,12},{12,14},{1,3},{3,5},{5,7},{... | collective-permute-start | bytes 589832 | tf_op jit(solution)/shard_map/ppermute | solution.py:22
  111.8 1.3 collective-permute-start.29
  113.4 4.8 %collective-permute-start.32 = (f32[2,3,2,32,128]{4,2,3,0,1:T(2,128)S(1)}, f32[2,3,2,32,128]{4,2,3,0,1:T(2,128)S(1)}, u32[]{:S(2)}, u32[]{:S(2)}) collective-permute-start(f32[2,3,2,32,128]{4,2,3,0,1:T(2,128)S(1)} %get-tuple-element.73), channel_id=1, source_target_pairs={{0,2},{2,4},{4,6},{6,8},{8,10},{10,12},{12,14},{1,3},{3,5},{5,7},{... | collective-permute-start | bytes 589832 | tf_op jit(solution)/shard_map/ppermute | solution.py:22
  118.2 1.5 collective-permute-start.33
  119.8 1.2 collective-permute-done.29
  121.0 1.3 collective-permute-start.30
  122.4 1.3 collective-permute-start.31
  123.7 5.9 %collective-permute-done.32 = f32[2,3,2,32,128]{4,2,3,0,1:T(2,128)S(1)} collective-permute-done((f32[2,3,2,32,128]{4,2,3,0,1:T(2,128)S(1)}, f32[2,3,2,32,128]{4,2,3,0,1:T(2,128)S(1)}, u32[]{:S(2)}, u32[]{:S(2)}) %collective-permute-start.32) | collective-permute-done | bytes 196640 | tf_op jit(solution)/shard_map/ppermute | solution.py:22
  129.6 1.9 collective-permute-start.34
  131.6 1.3 collective-permute-start.35
  133.8 0.8 collective-permute-done.35
  137.8 4.4 %collective-permute-start.36 = (f32[2,3,2,32,128]{4,2,3,0,1:T(2,128)S(1)}, f32[2,3,2,32,128]{4,2,3,0,1:T(2,128)S(1)}, u32[]{:S(2)}, u32[]{:S(2)}) collective-permute-start(f32[2,3,2,32,128]{4,2,3,0,1:T(2,128)S(1)} %get-tuple-element.46), channel_id=1, source_target_pairs={{0,2},{2,4},{4,6},{6,8},{8,10},{10,12},{12,14},{1,3},{3,5},{5,7},{... | collective-permute-start | bytes 589832 | tf_op jit(solution)/shard_map/ppermute | solution.py:22
  142.2 1.3 collective-permute-start.37
  143.8 5.3 %collective-permute-start.40 = (f32[2,3,2,32,128]{4,2,3,0,1:T(2,128)S(1)}, f32[2,3,2,32,128]{4,2,3,0,1:T(2,128)S(1)}, u32[]{:S(2)}, u32[]{:S(2)}) collective-permute-start(f32[2,3,2,32,128]{4,2,3,0,1:T(2,128)S(1)} %get-tuple-element.51), channel_id=1, source_target_pairs={{0,2},{2,4},{4,6},{6,8},{8,10},{10,12},{12,14},{1,3},{3,5},{5,7},{... | collective-permute-start | bytes 589832 | tf_op jit(solution)/shard_map/ppermute | solution.py:22
  149.1 1.3 collective-permute-start.41
  150.5 1.4 collective-permute-done.37
  152.0 1.3 collective-permute-start.38
  153.3 1.3 collective-permute-start.39
  154.6 5.9 %collective-permute-done.40 = f32[2,3,2,32,128]{4,2,3,0,1:T(2,128)S(1)} collective-permute-done((f32[2,3,2,32,128]{4,2,3,0,1:T(2,128)S(1)}, f32[2,3,2,32,128]{4,2,3,0,1:T(2,128)S(1)}, u32[]{:S(2)}, u32[]{:S(2)}) %collective-permute-start.40) | collective-permute-done | bytes 196640 | tf_op jit(solution)/shard_map/ppermute | solution.py:22
  160.6 1.9 collective-permute-start.42
  162.5 1.3 collective-permute-start.43
  164.8 0.8 collective-permute-done.43
  169.5 0.8 copy.51
  170.3 34.8 %psum.7 = f32[]{:T(128)} all-reduce(f32[]{:T(128)} %fusion.47), channel_id=1, replica_groups=mesh['cand'=2,'gx'=8,'gy'=2] {'gx','gy'}, use_global_device_ids=true, to_apply=%region_9.0 | all-reduce | flops 1 | bytes 8 | tf_op jit(solution)/shard_map/psum | solution.py:132
  206.6 0.8 copy.50
  (225 shorter events, 24.1 us)
Async XLA Ops:
  0.6 22.7 %copy-start = (f32[2,3,4,32,128]{4,3,2,1,0:T(8,128)S(1)}, f32[2,3,4,32,128]{4,3,2,1,0:T(8,128)}, u32[]{:S(2)}) copy-start(f32[2,3,4,32,128]{4,3,2,1,0:T(8,128)} %param.7) | copy-start | bytes 1179652
  1.7 36.1 %collective-permute-start.4 = (f32[2,32,128]{2,0,1:T(2,128)S(1)}, f32[2,32,128]{2,0,1:T(2,128)S(1)}, u32[]{:S(2)}, u32[]{:S(2)}) collective-permute-start(f32[2,32,128]{2,0,1:T(2,128)S(1)} %get-tuple-element.162), channel_id=1, source_target_pairs={{0,2},{2,4},{4,6},{6,8},{8,10},{10,12},{12,14},{1,3},{3,5},{5,7},{... | collective-permute-start | bytes 98312 | tf_op jit(solution)/shard_map/ppermute | solution.py:22
  6.6 32.5 %collective-permute-start.5 = (f32[2,32,128]{2,0,1:T(2,128)S(1)}, f32[2,32,128]{2,0,1:T(2,128)S(1)}, u32[]{:S(2)}, u32[]{:S(2)}) collective-permute-start(f32[2,32,128]{2,0,1:T(2,128)S(1)} %get-tuple-element.163), channel_id=1, source_target_pairs={{2,0},{4,2},{6,4},{8,6},{10,8},{12,10},{14,12},{3,1},{5,3},{7,5},{... | collective-permute-start | bytes 98312 | tf_op jit(solution)/shard_map/ppermute | solution.py:25
  10.8 20.8 %collective-permute-start.16 = (f32[2,32,128]{2,0,1:T(2,128)S(1)}, f32[2,32,128]{2,0,1:T(2,128)S(1)}, u32[]{:S(2)}, u32[]{:S(2)}) collective-permute-start(f32[2,32,128]{2,0,1:T(2,128)S(1)} %get-tuple-element.160), channel_id=1, source_target_pairs={{0,2},{2,4},{4,6},{6,8},{8,10},{10,12},{12,14},{1,3},{3,5},{5,7},{... | collective-permute-start | bytes 98312 | tf_op jit(solution)/shard_map/ppermute | solution.py:22
  16.2 8.8 %collective-permute-start.12 = (f32[2,32,128]{2,0,1:T(2,128)S(1)}, f32[2,32,128]{2,0,1:T(2,128)S(1)}, u32[]{:S(2)}, u32[]{:S(2)}) collective-permute-start(f32[2,32,128]{2,0,1:T(2,128)S(1)} %get-tuple-element.158), channel_id=1, source_target_pairs={{0,2},{2,4},{4,6},{6,8},{8,10},{10,12},{12,14},{1,3},{3,5},{5,7},{... | collective-permute-start | bytes 98312 | tf_op jit(solution)/shard_map/ppermute | solution.py:22
  20.6 5.8 %collective-permute-start.13 = (f32[2,32,128]{2,0,1:T(2,128)S(1)}, f32[2,32,128]{2,0,1:T(2,128)S(1)}, u32[]{:S(2)}, u32[]{:S(2)}) collective-permute-start(f32[2,32,128]{2,0,1:T(2,128)S(1)} %get-tuple-element.159), channel_id=1, source_target_pairs={{2,0},{4,2},{6,4},{8,6},{10,8},{12,10},{14,12},{3,1},{5,3},{7,5},{... | collective-permute-start | bytes 98312 | tf_op jit(solution)/shard_map/ppermute | solution.py:25
  21.9 0.7 copy-start.4
  23.3 1.0 copy-start.1
  25.0 11.4 %collective-permute-start.17 = (f32[2,32,128]{2,0,1:T(2,128)S(1)}, f32[2,32,128]{2,0,1:T(2,128)S(1)}, u32[]{:S(2)}, u32[]{:S(2)}) collective-permute-start(f32[2,32,128]{2,0,1:T(2,128)S(1)} %get-tuple-element.161), channel_id=1, source_target_pairs={{2,0},{4,2},{6,4},{8,6},{10,8},{12,10},{14,12},{3,1},{5,3},{7,5},{... | collective-permute-start | bytes 98312 | tf_op jit(solution)/shard_map/ppermute | solution.py:25
  26.4 38.6 %collective-permute-start.8 = (f32[2,3,2,32,128]{4,2,3,0,1:T(2,128)S(1)}, f32[2,3,2,32,128]{4,2,3,0,1:T(2,128)S(1)}, u32[]{:S(2)}, u32[]{:S(2)}) collective-permute-start(f32[2,3,2,32,128]{4,2,3,0,1:T(2,128)S(1)} %get-tuple-element.130), channel_id=1, source_target_pairs={{0,2},{2,4},{4,6},{6,8},{8,10},{10,12},{12,14},{1,3},{3,5},{5,7},{... | collective-permute-start | bytes 589832 | tf_op jit(solution)/shard_map/ppermute | solution.py:22
  31.6 29.0 %collective-permute-start = (f32[2,3,2,32,128]{4,2,3,0,1:T(2,128)S(1)}, f32[2,3,2,32,128]{4,2,3,0,1:T(2,128)S(1)}, u32[]{:S(2)}, u32[]{:S(2)}) collective-permute-start(f32[2,3,2,32,128]{4,2,3,0,1:T(2,128)S(1)} %get-tuple-element.128), channel_id=1, source_target_pairs={{0,2},{2,4},{4,6},{6,8},{8,10},{10,12},{12,14},{1,3},{3,5},{5,7},{... | collective-permute-start | bytes 589832 | tf_op jit(solution)/shard_map/ppermute | solution.py:22
  36.4 24.2 %collective-permute-start.1 = (f32[2,3,2,32,128]{4,2,3,0,1:T(2,128)S(1)}, f32[2,3,2,32,128]{4,2,3,0,1:T(2,128)S(1)}, u32[]{:S(2)}, u32[]{:S(2)}) collective-permute-start(f32[2,3,2,32,128]{4,2,3,0,1:T(2,128)S(1)} %get-tuple-element.129), channel_id=1, source_target_pairs={{2,0},{4,2},{6,4},{8,6},{10,8},{12,10},{14,12},{3,1},{5,3},{7,5},{... | collective-permute-start | bytes 589832 | tf_op jit(solution)/shard_map/ppermute | solution.py:25
  37.8 2.6 %collective-permute-start.18 = (f32[8,2,128]{2,0,1:T(8,128)S(1)}, f32[8,2,128]{2,0,1:T(8,128)S(1)}, u32[]{:S(2)}, u32[]{:S(2)}) collective-permute-start(f32[8,2,128]{2,0,1:T(8,128)S(1)} %get-tuple-element.152), channel_id=1, source_target_pairs={{0,1},{2,3},{4,5},{6,7},{8,9},{10,11},{12,13},{14,15},{16,17},{18,... | collective-permute-start | bytes 24584 | tf_op jit(solution)/shard_map/ppermute | solution.py:22
  39.1 4.4 %collective-permute-start.19 = (f32[8,2,128]{2,0,1:T(8,128)S(1)}, f32[8,2,128]{2,0,1:T(8,128)S(1)}, u32[]{:S(2)}, u32[]{:S(2)}) collective-permute-start(f32[8,2,128]{2,0,1:T(8,128)S(1)} %get-tuple-element.153), channel_id=1, source_target_pairs={{1,0},{3,2},{5,4},{7,6},{9,8},{11,10},{13,12},{15,14},{17,16},{19,... | collective-permute-start | bytes 24584 | tf_op jit(solution)/shard_map/ppermute | solution.py:25
  40.4 9.3 %collective-permute-start.14 = (f32[8,2,128]{2,0,1:T(8,128)S(1)}, f32[8,2,128]{2,0,1:T(8,128)S(1)}, u32[]{:S(2)}, u32[]{:S(2)}) collective-permute-start(f32[8,2,128]{2,0,1:T(8,128)S(1)} %get-tuple-element.148), channel_id=1, source_target_pairs={{0,1},{2,3},{4,5},{6,7},{8,9},{10,11},{12,13},{14,15},{16,17},{18,... | collective-permute-start | bytes 24584 | tf_op jit(solution)/shard_map/ppermute | solution.py:22
  43.5 9.3 %collective-permute-start.15 = (f32[8,2,128]{2,0,1:T(8,128)S(1)}, f32[8,2,128]{2,0,1:T(8,128)S(1)}, u32[]{:S(2)}, u32[]{:S(2)}) collective-permute-start(f32[8,2,128]{2,0,1:T(8,128)S(1)} %get-tuple-element.149), channel_id=1, source_target_pairs={{1,0},{3,2},{5,4},{7,6},{9,8},{11,10},{13,12},{15,14},{17,16},{19,... | collective-permute-start | bytes 24584 | tf_op jit(solution)/shard_map/ppermute | solution.py:25
  49.7 9.5 %collective-permute-start.6 = (f32[8,2,128]{2,0,1:T(8,128)S(1)}, f32[8,2,128]{2,0,1:T(8,128)S(1)}, u32[]{:S(2)}, u32[]{:S(2)}) collective-permute-start(f32[8,2,128]{2,0,1:T(8,128)S(1)} %get-tuple-element.156), channel_id=1, source_target_pairs={{0,1},{2,3},{4,5},{6,7},{8,9},{10,11},{12,13},{14,15},{16,17},{18,... | collective-permute-start | bytes 24584 | tf_op jit(solution)/shard_map/ppermute | solution.py:22
  52.8 7.8 %collective-permute-start.7 = (f32[8,2,128]{2,0,1:T(8,128)S(1)}, f32[8,2,128]{2,0,1:T(8,128)S(1)}, u32[]{:S(2)}, u32[]{:S(2)}) collective-permute-start(f32[8,2,128]{2,0,1:T(8,128)S(1)} %get-tuple-element.157), channel_id=1, source_target_pairs={{1,0},{3,2},{5,4},{7,6},{9,8},{11,10},{13,12},{15,14},{17,16},{19,... | collective-permute-start | bytes 24584 | tf_op jit(solution)/shard_map/ppermute | solution.py:25
  59.2 9.9 %collective-permute-start.9 = (f32[2,3,2,32,128]{4,2,3,0,1:T(2,128)S(1)}, f32[2,3,2,32,128]{4,2,3,0,1:T(2,128)S(1)}, u32[]{:S(2)}, u32[]{:S(2)}) collective-permute-start(f32[2,3,2,32,128]{4,2,3,0,1:T(2,128)S(1)} %get-tuple-element.131), channel_id=1, source_target_pairs={{2,0},{4,2},{6,4},{8,6},{10,8},{12,10},{14,12},{3,1},{5,3},{7,5},{... | collective-permute-start | bytes 589832 | tf_op jit(solution)/shard_map/ppermute | solution.py:25
  60.7 11.9 %collective-permute-start.2 = (f32[2,3,8,2,128]{4,2,3,0,1:T(8,128)S(1)}, f32[2,3,8,2,128]{4,2,3,0,1:T(8,128)S(1)}, u32[]{:S(2)}, u32[]{:S(2)}) collective-permute-start(f32[2,3,8,2,128]{4,2,3,0,1:T(8,128)S(1)} %get-tuple-element.124), channel_id=1, source_target_pairs={{0,1},{2,3},{4,5},{6,7},{8,9},{10,11},{12,13},{14,15},{16,17},{18,... | collective-permute-start | bytes 147464 | tf_op jit(solution)/shard_map/ppermute | solution.py:22
  63.7 8.9 %collective-permute-start.3 = (f32[2,3,8,2,128]{4,2,3,0,1:T(8,128)S(1)}, f32[2,3,8,2,128]{4,2,3,0,1:T(8,128)S(1)}, u32[]{:S(2)}, u32[]{:S(2)}) collective-permute-start(f32[2,3,8,2,128]{4,2,3,0,1:T(8,128)S(1)} %get-tuple-element.125), channel_id=1, source_target_pairs={{1,0},{3,2},{5,4},{7,6},{9,8},{11,10},{13,12},{15,14},{17,16},{19,... | collective-permute-start | bytes 147464 | tf_op jit(solution)/shard_map/ppermute | solution.py:25
  69.1 4.4 %collective-permute-start.10 = (f32[2,3,8,2,128]{4,2,3,0,1:T(8,128)S(1)}, f32[2,3,8,2,128]{4,2,3,0,1:T(8,128)S(1)}, u32[]{:S(2)}, u32[]{:S(2)}) collective-permute-start(f32[2,3,8,2,128]{4,2,3,0,1:T(8,128)S(1)} %get-tuple-element.126), channel_id=1, source_target_pairs={{0,1},{2,3},{4,5},{6,7},{8,9},{10,11},{12,13},{14,15},{16,17},{18,... | collective-permute-start | bytes 147464 | tf_op jit(solution)/shard_map/ppermute | solution.py:22
  71.3 3.1 %collective-permute-start.11 = (f32[2,3,8,2,128]{4,2,3,0,1:T(8,128)S(1)}, f32[2,3,8,2,128]{4,2,3,0,1:T(8,128)S(1)}, u32[]{:S(2)}, u32[]{:S(2)}) collective-permute-start(f32[2,3,8,2,128]{4,2,3,0,1:T(8,128)S(1)} %get-tuple-element.127), channel_id=1, source_target_pairs={{1,0},{3,2},{5,4},{7,6},{9,8},{11,10},{13,12},{15,14},{17,16},{19,... | collective-permute-start | bytes 147464 | tf_op jit(solution)/shard_map/ppermute | solution.py:25
  77.5 14.5 %collective-permute-start.20 = (f32[2,3,2,32,128]{4,2,3,0,1:T(2,128)S(1)}, f32[2,3,2,32,128]{4,2,3,0,1:T(2,128)S(1)}, u32[]{:S(2)}, u32[]{:S(2)}) collective-permute-start(f32[2,3,2,32,128]{4,2,3,0,1:T(2,128)S(1)} %get-tuple-element.90), channel_id=1, source_target_pairs={{0,2},{2,4},{4,6},{6,8},{8,10},{10,12},{12,14},{1,3},{3,5},{5,7},{... | collective-permute-start | bytes 589832 | tf_op jit(solution)/shard_map/ppermute | solution.py:22
  82.5 9.5 %collective-permute-start.21 = (f32[2,3,2,32,128]{4,2,3,0,1:T(2,128)S(1)}, f32[2,3,2,32,128]{4,2,3,0,1:T(2,128)S(1)}, u32[]{:S(2)}, u32[]{:S(2)}) collective-permute-start(f32[2,3,2,32,128]{4,2,3,0,1:T(2,128)S(1)} %get-tuple-element.91), channel_id=1, source_target_pairs={{2,0},{4,2},{6,4},{8,6},{10,8},{12,10},{14,12},{3,1},{5,3},{7,5},{... | collective-permute-start | bytes 589832 | tf_op jit(solution)/shard_map/ppermute | solution.py:25
  84.1 15.6 %collective-permute-start.24 = (f32[2,3,2,32,128]{4,2,3,0,1:T(2,128)S(1)}, f32[2,3,2,32,128]{4,2,3,0,1:T(2,128)S(1)}, u32[]{:S(2)}, u32[]{:S(2)}) collective-permute-start(f32[2,3,2,32,128]{4,2,3,0,1:T(2,128)S(1)} %get-tuple-element.95), channel_id=1, source_target_pairs={{0,2},{2,4},{4,6},{6,8},{8,10},{10,12},{12,14},{1,3},{3,5},{5,7},{... | collective-permute-start | bytes 589832 | tf_op jit(solution)/shard_map/ppermute | solution.py:22
  88.7 11.1 %collective-permute-start.25 = (f32[2,3,2,32,128]{4,2,3,0,1:T(2,128)S(1)}, f32[2,3,2,32,128]{4,2,3,0,1:T(2,128)S(1)}, u32[]{:S(2)}, u32[]{:S(2)}) collective-permute-start(f32[2,3,2,32,128]{4,2,3,0,1:T(2,128)S(1)} %get-tuple-element.96), channel_id=1, source_target_pairs={{2,0},{4,2},{6,4},{8,6},{10,8},{12,10},{14,12},{3,1},{5,3},{7,5},{... | collective-permute-start | bytes 589832 | tf_op jit(solution)/shard_map/ppermute | solution.py:25
  92.0 10.4 %collective-permute-start.22 = (f32[2,3,8,2,128]{4,2,3,0,1:T(8,128)S(1)}, f32[2,3,8,2,128]{4,2,3,0,1:T(8,128)S(1)}, u32[]{:S(2)}, u32[]{:S(2)}) collective-permute-start(f32[2,3,8,2,128]{4,2,3,0,1:T(8,128)S(1)} %get-tuple-element.120), channel_id=1, source_target_pairs={{0,1},{2,3},{4,5},{6,7},{8,9},{10,11},{12,13},{14,15},{16,17},{18,... | collective-permute-start | bytes 147464 | tf_op jit(solution)/shard_map/ppermute | solution.py:22
  93.3 9.1 %collective-permute-start.23 = (f32[2,3,8,2,128]{4,2,3,0,1:T(8,128)S(1)}, f32[2,3,8,2,128]{4,2,3,0,1:T(8,128)S(1)}, u32[]{:S(2)}, u32[]{:S(2)}) collective-permute-start(f32[2,3,8,2,128]{4,2,3,0,1:T(8,128)S(1)} %get-tuple-element.121), channel_id=1, source_target_pairs={{1,0},{3,2},{5,4},{7,6},{9,8},{11,10},{13,12},{15,14},{17,16},{19,... | collective-permute-start | bytes 147464 | tf_op jit(solution)/shard_map/ppermute | solution.py:25
  99.8 3.6 %collective-permute-start.26 = (f32[2,3,8,2,128]{4,2,3,0,1:T(8,128)S(1)}, f32[2,3,8,2,128]{4,2,3,0,1:T(8,128)S(1)}, u32[]{:S(2)}, u32[]{:S(2)}) collective-permute-start(f32[2,3,8,2,128]{4,2,3,0,1:T(8,128)S(1)} %get-tuple-element.122), channel_id=1, source_target_pairs={{0,1},{2,3},{4,5},{6,7},{8,9},{10,11},{12,13},{14,15},{16,17},{18,... | collective-permute-start | bytes 147464 | tf_op jit(solution)/shard_map/ppermute | solution.py:22
  101.1 3.1 %collective-permute-start.27 = (f32[2,3,8,2,128]{4,2,3,0,1:T(8,128)S(1)}, f32[2,3,8,2,128]{4,2,3,0,1:T(8,128)S(1)}, u32[]{:S(2)}, u32[]{:S(2)}) collective-permute-start(f32[2,3,8,2,128]{4,2,3,0,1:T(8,128)S(1)} %get-tuple-element.123), channel_id=1, source_target_pairs={{1,0},{3,2},{5,4},{7,6},{9,8},{11,10},{13,12},{15,14},{17,16},{19,... | collective-permute-start | bytes 147464 | tf_op jit(solution)/shard_map/ppermute | solution.py:25
  107.4 12.4 %collective-permute-start.28 = (f32[2,3,2,32,128]{4,2,3,0,1:T(2,128)S(1)}, f32[2,3,2,32,128]{4,2,3,0,1:T(2,128)S(1)}, u32[]{:S(2)}, u32[]{:S(2)}) collective-permute-start(f32[2,3,2,32,128]{4,2,3,0,1:T(2,128)S(1)} %get-tuple-element.68), channel_id=1, source_target_pairs={{0,2},{2,4},{4,6},{6,8},{8,10},{10,12},{12,14},{1,3},{3,5},{5,7},{... | collective-permute-start | bytes 589832 | tf_op jit(solution)/shard_map/ppermute | solution.py:22
  111.8 9.2 %collective-permute-start.29 = (f32[2,3,2,32,128]{4,2,3,0,1:T(2,128)S(1)}, f32[2,3,2,32,128]{4,2,3,0,1:T(2,128)S(1)}, u32[]{:S(2)}, u32[]{:S(2)}) collective-permute-start(f32[2,3,2,32,128]{4,2,3,0,1:T(2,128)S(1)} %get-tuple-element.69), channel_id=1, source_target_pairs={{2,0},{4,2},{6,4},{8,6},{10,8},{12,10},{14,12},{3,1},{5,3},{7,5},{... | collective-permute-start | bytes 589832 | tf_op jit(solution)/shard_map/ppermute | solution.py:25
  113.4 16.2 %collective-permute-start.32 = (f32[2,3,2,32,128]{4,2,3,0,1:T(2,128)S(1)}, f32[2,3,2,32,128]{4,2,3,0,1:T(2,128)S(1)}, u32[]{:S(2)}, u32[]{:S(2)}) collective-permute-start(f32[2,3,2,32,128]{4,2,3,0,1:T(2,128)S(1)} %get-tuple-element.73), channel_id=1, source_target_pairs={{0,2},{2,4},{4,6},{6,8},{8,10},{10,12},{12,14},{1,3},{3,5},{5,7},{... | collective-permute-start | bytes 589832 | tf_op jit(solution)/shard_map/ppermute | solution.py:22
  118.2 11.4 %collective-permute-start.33 = (f32[2,3,2,32,128]{4,2,3,0,1:T(2,128)S(1)}, f32[2,3,2,32,128]{4,2,3,0,1:T(2,128)S(1)}, u32[]{:S(2)}, u32[]{:S(2)}) collective-permute-start(f32[2,3,2,32,128]{4,2,3,0,1:T(2,128)S(1)} %get-tuple-element.74), channel_id=1, source_target_pairs={{2,0},{4,2},{6,4},{8,6},{10,8},{12,10},{14,12},{3,1},{5,3},{7,5},{... | collective-permute-start | bytes 589832 | tf_op jit(solution)/shard_map/ppermute | solution.py:25
  121.0 11.8 %collective-permute-start.30 = (f32[2,3,8,2,128]{4,2,3,0,1:T(8,128)S(1)}, f32[2,3,8,2,128]{4,2,3,0,1:T(8,128)S(1)}, u32[]{:S(2)}, u32[]{:S(2)}) collective-permute-start(f32[2,3,8,2,128]{4,2,3,0,1:T(8,128)S(1)} %get-tuple-element.116), channel_id=1, source_target_pairs={{0,1},{2,3},{4,5},{6,7},{8,9},{10,11},{12,13},{14,15},{16,17},{18,... | collective-permute-start | bytes 147464 | tf_op jit(solution)/shard_map/ppermute | solution.py:22
  122.4 10.5 %collective-permute-start.31 = (f32[2,3,8,2,128]{4,2,3,0,1:T(8,128)S(1)}, f32[2,3,8,2,128]{4,2,3,0,1:T(8,128)S(1)}, u32[]{:S(2)}, u32[]{:S(2)}) collective-permute-start(f32[2,3,8,2,128]{4,2,3,0,1:T(8,128)S(1)} %get-tuple-element.117), channel_id=1, source_target_pairs={{1,0},{3,2},{5,4},{7,6},{9,8},{11,10},{13,12},{15,14},{17,16},{19,... | collective-permute-start | bytes 147464 | tf_op jit(solution)/shard_map/ppermute | solution.py:25
  129.6 4.2 %collective-permute-start.34 = (f32[2,3,8,2,128]{4,2,3,0,1:T(8,128)S(1)}, f32[2,3,8,2,128]{4,2,3,0,1:T(8,128)S(1)}, u32[]{:S(2)}, u32[]{:S(2)}) collective-permute-start(f32[2,3,8,2,128]{4,2,3,0,1:T(8,128)S(1)} %get-tuple-element.118), channel_id=1, source_target_pairs={{0,1},{2,3},{4,5},{6,7},{8,9},{10,11},{12,13},{14,15},{16,17},{18,... | collective-permute-start | bytes 147464 | tf_op jit(solution)/shard_map/ppermute | solution.py:22
  131.6 3.1 %collective-permute-start.35 = (f32[2,3,8,2,128]{4,2,3,0,1:T(8,128)S(1)}, f32[2,3,8,2,128]{4,2,3,0,1:T(8,128)S(1)}, u32[]{:S(2)}, u32[]{:S(2)}) collective-permute-start(f32[2,3,8,2,128]{4,2,3,0,1:T(8,128)S(1)} %get-tuple-element.119), channel_id=1, source_target_pairs={{1,0},{3,2},{5,4},{7,6},{9,8},{11,10},{13,12},{15,14},{17,16},{19,... | collective-permute-start | bytes 147464 | tf_op jit(solution)/shard_map/ppermute | solution.py:25
  137.8 12.7 %collective-permute-start.36 = (f32[2,3,2,32,128]{4,2,3,0,1:T(2,128)S(1)}, f32[2,3,2,32,128]{4,2,3,0,1:T(2,128)S(1)}, u32[]{:S(2)}, u32[]{:S(2)}) collective-permute-start(f32[2,3,2,32,128]{4,2,3,0,1:T(2,128)S(1)} %get-tuple-element.46), channel_id=1, source_target_pairs={{0,2},{2,4},{4,6},{6,8},{8,10},{10,12},{12,14},{1,3},{3,5},{5,7},{... | collective-permute-start | bytes 589832 | tf_op jit(solution)/shard_map/ppermute | solution.py:22
  142.2 9.8 %collective-permute-start.37 = (f32[2,3,2,32,128]{4,2,3,0,1:T(2,128)S(1)}, f32[2,3,2,32,128]{4,2,3,0,1:T(2,128)S(1)}, u32[]{:S(2)}, u32[]{:S(2)}) collective-permute-start(f32[2,3,2,32,128]{4,2,3,0,1:T(2,128)S(1)} %get-tuple-element.47), channel_id=1, source_target_pairs={{2,0},{4,2},{6,4},{8,6},{10,8},{12,10},{14,12},{3,1},{5,3},{7,5},{... | collective-permute-start | bytes 589832 | tf_op jit(solution)/shard_map/ppermute | solution.py:25
  143.8 16.7 %collective-permute-start.40 = (f32[2,3,2,32,128]{4,2,3,0,1:T(2,128)S(1)}, f32[2,3,2,32,128]{4,2,3,0,1:T(2,128)S(1)}, u32[]{:S(2)}, u32[]{:S(2)}) collective-permute-start(f32[2,3,2,32,128]{4,2,3,0,1:T(2,128)S(1)} %get-tuple-element.51), channel_id=1, source_target_pairs={{0,2},{2,4},{4,6},{6,8},{8,10},{10,12},{12,14},{1,3},{3,5},{5,7},{... | collective-permute-start | bytes 589832 | tf_op jit(solution)/shard_map/ppermute | solution.py:22
  149.1 11.4 %collective-permute-start.41 = (f32[2,3,2,32,128]{4,2,3,0,1:T(2,128)S(1)}, f32[2,3,2,32,128]{4,2,3,0,1:T(2,128)S(1)}, u32[]{:S(2)}, u32[]{:S(2)}) collective-permute-start(f32[2,3,2,32,128]{4,2,3,0,1:T(2,128)S(1)} %get-tuple-element.52), channel_id=1, source_target_pairs={{2,0},{4,2},{6,4},{8,6},{10,8},{12,10},{14,12},{3,1},{5,3},{7,5},{... | collective-permute-start | bytes 589832 | tf_op jit(solution)/shard_map/ppermute | solution.py:25
  152.0 11.8 %collective-permute-start.38 = (f32[2,3,8,2,128]{4,2,3,0,1:T(8,128)S(1)}, f32[2,3,8,2,128]{4,2,3,0,1:T(8,128)S(1)}, u32[]{:S(2)}, u32[]{:S(2)}) collective-permute-start(f32[2,3,8,2,128]{4,2,3,0,1:T(8,128)S(1)} %get-tuple-element.112), channel_id=1, source_target_pairs={{0,1},{2,3},{4,5},{6,7},{8,9},{10,11},{12,13},{14,15},{16,17},{18,... | collective-permute-start | bytes 147464 | tf_op jit(solution)/shard_map/ppermute | solution.py:22
  153.3 10.5 %collective-permute-start.39 = (f32[2,3,8,2,128]{4,2,3,0,1:T(8,128)S(1)}, f32[2,3,8,2,128]{4,2,3,0,1:T(8,128)S(1)}, u32[]{:S(2)}, u32[]{:S(2)}) collective-permute-start(f32[2,3,8,2,128]{4,2,3,0,1:T(8,128)S(1)} %get-tuple-element.113), channel_id=1, source_target_pairs={{1,0},{3,2},{5,4},{7,6},{9,8},{11,10},{13,12},{15,14},{17,16},{19,... | collective-permute-start | bytes 147464 | tf_op jit(solution)/shard_map/ppermute | solution.py:25
  160.6 4.2 %collective-permute-start.42 = (f32[2,3,8,2,128]{4,2,3,0,1:T(8,128)S(1)}, f32[2,3,8,2,128]{4,2,3,0,1:T(8,128)S(1)}, u32[]{:S(2)}, u32[]{:S(2)}) collective-permute-start(f32[2,3,8,2,128]{4,2,3,0,1:T(8,128)S(1)} %get-tuple-element.114), channel_id=1, source_target_pairs={{0,1},{2,3},{4,5},{6,7},{8,9},{10,11},{12,13},{14,15},{16,17},{18,... | collective-permute-start | bytes 147464 | tf_op jit(solution)/shard_map/ppermute | solution.py:22
  162.5 3.1 %collective-permute-start.43 = (f32[2,3,8,2,128]{4,2,3,0,1:T(8,128)S(1)}, f32[2,3,8,2,128]{4,2,3,0,1:T(8,128)S(1)}, u32[]{:S(2)}, u32[]{:S(2)}) collective-permute-start(f32[2,3,8,2,128]{4,2,3,0,1:T(8,128)S(1)} %get-tuple-element.115), channel_id=1, source_target_pairs={{1,0},{3,2},{5,4},{7,6},{9,8},{11,10},{13,12},{15,14},{17,16},{19,... | collective-permute-start | bytes 147464 | tf_op jit(solution)/shard_map/ppermute | solution.py:25
  169.5 36.3 %copy-start.2 = (f32[4,32,128]{2,1,0:T(8,128)S(1)}, f32[4,32,128]{2,1,0:T(8,128)}, u32[]{:S(2)}) copy-start(f32[4,32,128]{2,1,0:T(8,128)} %param.9) | copy-start | bytes 196612
  169.5 36.3 %copy-start.3 = (s32[4,32,128]{2,1,0:T(8,128)S(1)}, s32[4,32,128]{2,1,0:T(8,128)}, u32[]{:S(2)}) copy-start(s32[4,32,128]{2,1,0:T(8,128)} %param.10) | copy-start | bytes 196612
where the time goes:
time: 209 us; the launch traced here: 207 us
  starting transfers between devices  102 us (49%)
  blocking collectives  34.8 us (17%)
  waiting for transfers between devices  29.1 us (14%)
  other arithmetic  24.6 us (12%)
  local copies, waits for them, and re-layouts  13.3 us (6%)
  between operations  3.08 us (1%)
    ppermute x22, starting transfers between devices, with_halo(): lax.ppermute(lax.slice_in_dim(block, block.shape[dim] - width, None, axis...  73.8 us
    psum x1, blocking collectives, shards(): power = lax.psum(local_power, ('gx', 'gy')) / (total_x * total_y)  34.8 us
    ppermute x22, starting transfers between devices, with_halo(): lax.ppermute(lax.slice_in_dim(block, 0, width, axis=dim), axis, backward)  28.6 us
    ppermute x22, waiting for transfers between devices, with_halo(): lax.ppermute(lax.slice_in_dim(block, block.shape[dim] - width, None, axis...  18.8 us
    ppermute x22, waiting for transfers between devices, with_halo(): lax.ppermute(lax.slice_in_dim(block, 0, width, axis=dim), axis, backward)  10.3 us
    mul x2, other arithmetic, shards(): source_wide * waveforms[0, step]  5.12 us
    mul x2, other arithmetic, shards(): adjoint_wide * waveforms[1, step]  4.94 us
  transfers between devices with their start and end apart: 44, of which 12 were waited for; matrix products, arithmetic and copies ran while one was open for 10% of the time, Pallas kernels for 0%

commit v1 on v0

v1 whole, which is shorter than its diff:
```python
import functools

import jax
import jax.numpy as jnp
from jax import lax
from jax.experimental import pallas as pl
from jax.experimental.pallas import tpu as pltpu
from jax.sharding import PartitionSpec as P

STEPS = 8
PMLW = 8
TILE = 8

step_dt = 0.7
contrast = 5.0
sigma_max = 2.0
small_eps = 1e-06
inv_spacing = 0.5

MESH = pl.DeviceIdType.MESH


def coefficients(depth_cells, layer):
    zpos = lax.broadcasted_iota(jnp.int32, (1, depth_cells), 1).astype(jnp.float32)
    lower = (layer - zpos - 0.5) / layer
    upper = (zpos + 0.5 - (depth_cells - layer)) / layer
    depth = jnp.maximum(jnp.maximum(lower, upper), 0.0)
    sigma = sigma_max * depth * depth * depth
    half = sigma * step_dt / 2.0
    return ((1.0 - half) / (1.0 + half), step_dt / (1.0 + half))


def kernel(
    count_x,
    count_y,
    electric,
    magnetic,
    density,
    mask,
    planes,
    profiles,
    waves,
    electric_out,
    magnetic_out,
    gradient_out,
    elec,
    magn,
    scaled,
    source,
    corr,
    front,
    send_up,
    send_down,
    from_low,
    from_high,
    power_mine,
    power_all,
    grad,
    load_sem,
    store_sem,
    side_send,
    side_recv,
    first_send,
    first_recv,
    up_send,
    up_recv,
    down_send,
    down_recv,
    power_send,
    power_recv,
):
    sets, comps, wx, wy, depth_z = electric.shape
    rows = wy + TILE
    last = wx - 1
    gx = lax.axis_index("gx")
    gy = lax.axis_index("gy")
    group = count_x * count_y
    me = gx * count_y + gy
    other = {"gy": 1 - gy}
    upper = {"gx": lax.rem(gx + 1, count_x)}
    lower = {"gx": lax.rem(gx + count_x - 1, count_x)}
    own = pl.multiple_of(gy * TILE, TILE)

    def peer(j):
        at = lax.rem(me + j, group)
        return at, {"gx": at // count_y, "gy": lax.rem(at, count_y)}

    barrier = pltpu.get_barrier_semaphore()

    def greet(j, carry):
        pl.semaphore_signal(barrier, inc=1, device_id=peer(j)[1], device_id_type=MESH)
        return carry

    lax.fori_loop(1, group, greet, 0)

    loads = [
        pltpu.make_async_copy(electric, elec.at[:, :, :, pl.ds(own, wy), :], load_sem.at[0]),
        pltpu.make_async_copy(
            magnetic, magn.at[:, :, pl.ds(1, wx), pl.ds(own + TILE, wy), :], load_sem.at[1]
        ),
    ]
    for load in loads:
        load.start()

    elec[:, :, :, rows:, :] = jnp.zeros((sets, comps, wx, TILE, depth_z), jnp.float32)
    magn[:, :, 1:, :TILE, :] = jnp.zeros((sets, comps, wx, TILE, depth_z), jnp.float32)

    @pl.when(gx == 0)
    def _():
        magn[:, 1:, 0, TILE:, :] = jnp.zeros((sets, comps - 1, rows, depth_z), jnp.float32)

    corr[...] = jnp.zeros_like(corr)
    decay, gain = coefficients(depth_z, PMLW)
    gain_half = gain * inv_spacing
    lane = lax.broadcasted_iota(jnp.int32, (1, depth_z), 1)
    flags = mask[...].astype(jnp.float32)
    inv_eps = 1.0 / (1.0 + contrast * density[...] * flags)
    front[...] = flags * contrast * inv_eps * inv_eps * step_dt
    scaled[:, pl.ds(own, wy), :] = inv_eps * gain
    eye = lax.broadcasted_iota(jnp.int32, (wy, wy), 0) == lax.broadcasted_iota(
        jnp.int32, (wy, wy), 1
    )
    for s in range(sets):
        hot = jnp.where(lane == planes[s], gain, 0.0)
        for x in range(wx):
            row = jnp.broadcast_to(profiles[s, x : x + 1, :], (wy, wy))
            column = jnp.sum(jnp.where(eye, row, 0.0), axis=1, keepdims=True)
            source[s, x, pl.ds(own, wy), :] = column * hot

    for load in loads:
        load.wait()
    pl.semaphore_wait(barrier, group - 1)

    take = pl.multiple_of((1 - gy) * (wy - TILE) + gy * TILE, TILE)
    put = pl.multiple_of(gy * wy, TILE)
    spots = [
        (elec, (slice(None),) * 3, 0),
        (magn, (slice(None), slice(None), pl.ds(1, wx)), TILE),
        (scaled, (slice(None),), 0),
        (source, (slice(None),) * 2, 0),
    ]
    sides = [
        pltpu.make_async_remote_copy(
            src_ref=ref.at[(*lead, pl.ds(take + base, TILE), slice(None))],
            dst_ref=ref.at[(*lead, pl.ds(put + base, TILE), slice(None))],
            send_sem=side_send.at[k],
            recv_sem=side_recv.at[k],
            device_id=other,
            device_id_type=MESH,
        )
        for k, (ref, lead, base) in enumerate(spots)
    ]
    for side in sides:
        side.start()
    for side in sides:
        side.wait()

    def next_z(f):
        return jnp.where(lane < depth_z - 1, pltpu.roll(f, depth_z - 1, 1), 0.0)

    def previous_z(f):
        return jnp.where(lane > 0, pltpu.roll(f, 1, 1), 0.0)

    def up_copy(e, s):
        return pltpu.make_async_remote_copy(
            src_ref=send_up.at[e, s],
            dst_ref=from_low.at[e, s],
            send_sem=up_send.at[e, s],
            recv_sem=up_recv.at[e, s],
            device_id=upper,
            device_id_type=MESH,
        )

    def down_copy(e, s):
        return pltpu.make_async_remote_copy(
            src_ref=send_down.at[e, s],
            dst_ref=from_high.at[e, s],
            send_sem=down_send.at[e, s],
            recv_sem=down_recv.at[e, s],
            device_id=lower,
            device_id_type=MESH,
        )

    def first_copy(s):
        return pltpu.make_async_remote_copy(
            src_ref=magn.at[s, pl.ds(1, 2), wx, pl.ds(TILE, rows), :],
            dst_ref=magn.at[s, pl.ds(1, 2), 0, pl.ds(TILE, rows), :],
            send_sem=first_send.at[s],
            recv_sem=first_recv.at[s],
            device_id=upper,
            device_id_type=MESH,
        )

    def send(e, s):
        ex = elec[s, 0, last, :rows, :]
        send_up[e, s, 0] = (next_z(ex) - ex) * inv_spacing + elec[s, 2, last, :rows, :]
        send_up[e, s, 1] = (elec[s, 0, last, 1 : rows + 1, :] - ex) * inv_spacing + elec[
            s, 1, last, :rows, :
        ]
        send_down[e, s, 0] = elec[s, 1, 0, :rows, :]
        send_down[e, s, 1] = elec[s, 2, 0, :rows, :]

        @pl.when(gx < count_x - 1)
        def _():
            up_copy(e, s).start()

        @pl.when(gx > 0)
        def _():
            down_copy(e, s).start()

    def magnetic_at(s, x, ey_next, ez_next):
        ex = elec[s, 0, x, :rows, :]
        ey = elec[s, 1, x, :rows, :]
        ez = elec[s, 2, x, :rows, :]
        ex_y = elec[s, 0, x, 1 : rows + 1, :]
        ez_y = elec[s, 2, x, 1 : rows + 1, :]
        hx = magn[s, 0, x + 1, TILE:, :]
        hy = magn[s, 1, x + 1, TILE:, :]
        hz = magn[s, 2, x + 1, TILE:, :]
        magn[s, 0, x + 1, TILE:, :] = decay * hx - gain_half * ((ez_y - ez) - (next_z(ey) - ey))
        magn[s, 1, x + 1, TILE:, :] = (
            decay * hy - gain_half * (next_z(ex) - ex) + gain * (ez_next - ez)
        )
        magn[s, 2, x + 1, TILE:, :] = (
            decay * hz - gain * (ey_next - ey) + gain_half * (ex_y - ex)
        )

    def electric_at(t, s, x):
        hx = magn[s, 0, x + 1, TILE:, :]
        hy = magn[s, 1, x + 1, TILE:, :]
        hz = magn[s, 2, x + 1, TILE:, :]
        hx_y = magn[s, 0, x + 1, TILE - 1 : TILE - 1 + rows, :]
        hz_y = magn[s, 2, x + 1, TILE - 1 : TILE - 1 + rows, :]
        hy_x = magn[s, 1, x, TILE:, :]
        hz_x = magn[s, 2, x, TILE:, :]
        weight = scaled[x]
        half = weight * inv_spacing
        elec[s, 0, x, :rows, :] = (
            decay * elec[s, 0, x, :rows, :]
            + half * ((hz - hz_y) - (hy - previous_z(hy)))
            - source[s, x] * waves[s, t]
        )
        elec[s, 1, x, :rows, :] = (
            decay * elec[s, 1, x, :rows, :]
            + half * (hx - previous_z(hx))
            - weight * (hz - hz_x)
        )
        elec[s, 2, x, :rows, :] = (
            decay * elec[s, 2, x, :rows, :] + weight * (hy - hy_x) - half * (hx - hx_y)
        )

    def inner(t, s):
        for x in range(last):
            magnetic_at(s, x, elec[s, 1, x + 1, :rows, :], elec[s, 2, x + 1, :rows, :])
        for x in range(1, last):
            electric_at(t, s, x)

    def outer(t, s):
        @pl.when(gx > 0)
        def _():
            up_copy(t, s).wait_recv()

        @pl.when(gx < count_x - 1)
        def _():
            down_copy(t, s).wait_recv()

        inside = jnp.where(gx < count_x - 1, 1, 0)
        keep = jnp.broadcast_to(inside, (rows, depth_z)) == 1
        magnetic_at(
            s,
            last,
            jnp.where(keep, from_high[t, s, 0], 0.0),
            jnp.where(keep, from_high[t, s, 1], 0.0),
        )
        hy = magn[s, 1, 0, TILE:, :]
        hz = magn[s, 2, 0, TILE:, :]
        there = jnp.broadcast_to(jnp.where(gx > 0, 1, 0), (rows, depth_z)) == 1
        magn[s, 1, 0, TILE:, :] = jnp.where(
            there, decay * hy - gain * (from_low[t, s, 0] - elec[s, 2, 0, :rows, :]), 0.0
        )
        magn[s, 2, 0, TILE:, :] = jnp.where(
            there, decay * hz - gain * (elec[s, 1, 0, :rows, :] - from_low[t, s, 1]), 0.0
        )
        electric_at(t, s, 0)
        if last > 0:
            electric_at(t, s, last)

    def correlate():
        for x in range(wx):
            total = corr[x]
            for c in range(comps):
                total = total + elec[0, c, x, :rows, :] * elec[1, c, x, :rows, :]
            corr[x] = total

    for s in range(sets):
        send(0, s)

        @pl.when(gx < count_x - 1)
        def _():
            first_copy(s).start()

    for s in range(sets):
        inner(0, s)

    for s in range(sets):

        @pl.when(gx > 0)
        def _():
            first_copy(s).wait_recv()

        @pl.when(gx < count_x - 1)
        def _():
            first_copy(s).wait_send()

    def step(t, carry):
        for s in range(sets):
            outer(t, s)
            send(t + 1, s)
        correlate()
        for s in range(sets):
            inner(t + 1, s)
        return carry

    lax.fori_loop(0, STEPS - 1, step, 0)

    def give(s):
        return [
            pltpu.make_async_copy(
                elec.at[s, :, :, pl.ds(own, wy), :], electric_out.at[s], store_sem.at[0, s]
            ),
            pltpu.make_async_copy(
                magn.at[s, :, pl.ds(1, wx), pl.ds(own + TILE, wy), :],
                magnetic_out.at[s],
                store_sem.at[1, s],
            ),
        ]

    def power_copy(j, sender):
        at, device = peer(j)
        return pltpu.make_async_remote_copy(
            src_ref=power_mine,
            dst_ref=power_all.at[sender],
            send_sem=power_send.at[at],
            recv_sem=power_recv.at[sender],
            device_id=device,
            device_id_type=MESH,
        )

    outer(STEPS - 1, 0)
    local = jnp.zeros((TILE, depth_z), jnp.float32)
    for c in range(comps):
        for x in range(wx):
            field = elec[0, c, x, pl.ds(own, wy), :]
            square = field * field
            for k in range(wy // TILE):
                local = local + square[k * TILE : (k + 1) * TILE, :]
    local = jnp.where(lane == planes[1], local, 0.0)
    power_mine[...] = local
    power_all[me] = local

    def share(j, carry):
        power_copy(j, me).start()
        return carry

    lax.fori_loop(1, group, share, 0)
    for copy in give(0):
        copy.start()

    outer(STEPS - 1, 1)
    for copy in give(1):
        copy.start()
    correlate()

    def collect(j, carry):
        at, _ = peer(j)
        power_copy(j, at).wait_recv()
        return carry

    lax.fori_loop(1, group, collect, 0)

    def add(j, total):
        return total + power_all[j]

    total = lax.fori_loop(0, group, add, jnp.zeros((TILE, depth_z), jnp.float32))
    power = jnp.sum(jnp.sum(total, axis=0, keepdims=True), axis=1, keepdims=True)
    power = power / (wx * count_x * wy * count_y)
    scale = 1.0 / (power + small_eps)
    for x in range(wx):
        grad[x] = front[x] * corr[x, pl.ds(own, wy), :] * scale
    last_copy = pltpu.make_async_copy(grad, gradient_out, load_sem.at[0])
    last_copy.start()

    def sent(j, carry):
        power_copy(j, me).wait_send()
        return carry

    lax.fori_loop(1, group, sent, 0)

    def drain(e, carry):
        for s in range(sets):

            @pl.when(gx < count_x - 1)
            def _():
                up_copy(e, s).wait_send()

            @pl.when(gx > 0)
            def _():
                down_copy(e, s).wait_send()

        return carry

    lax.fori_loop(0, STEPS, drain, 0)
    for s in range(sets):
        for copy in give(s):
            copy.wait()
    last_copy.wait()


def shards(count_x, count_y, electric, magnetic, density, design_mask, planes, profiles, waveforms):
    sets, comps, wx, wy, depth_z = electric.shape
    assert count_y == 2 and STEPS <= TILE
    rows = wy + TILE
    group = count_x * count_y
    f32 = jnp.float32
    dma = pltpu.SemaphoreType.DMA
    hbm = pl.BlockSpec(memory_space=pl.ANY)
    vmem = pl.BlockSpec(memory_space=pltpu.VMEM)
    smem = pl.BlockSpec(memory_space=pltpu.SMEM)
    return pl.pallas_call(
        functools.partial(kernel, count_x, count_y),
        out_shape=(
            jax.ShapeDtypeStruct(electric.shape, f32),
            jax.ShapeDtypeStruct(magnetic.shape, f32),
            jax.ShapeDtypeStruct(density.shape, f32),
        ),
        in_specs=[hbm, hbm, vmem, vmem, smem, vmem, smem],
        out_specs=(hbm, hbm, hbm),
        scratch_shapes=[
            pltpu.VMEM((sets, comps, wx, rows + TILE, depth_z), f32),
            pltpu.VMEM((sets, comps, wx + 1, rows + TILE, depth_z), f32),
            pltpu.VMEM((wx, rows, depth_z), f32),
            pltpu.VMEM((sets, wx, rows, depth_z), f32),
            pltpu.VMEM((wx, rows, depth_z), f32),
            pltpu.VMEM((wx, wy, depth_z), f32),
            pltpu.VMEM((STEPS, sets, 2, rows, depth_z), f32),
            pltpu.VMEM((STEPS, sets, 2, rows, depth_z), f32),
            pltpu.VMEM((STEPS, sets, 2, rows, depth_z), f32),
            pltpu.VMEM((STEPS, sets, 2, rows, depth_z), f32),
            pltpu.VMEM((TILE, depth_z), f32),
            pltpu.VMEM((group, TILE, depth_z), f32),
            pltpu.VMEM((wx, wy, depth_z), f32),
            dma((2,)),
            dma((2, sets)),
            dma((4,)),
            dma((4,)),
            dma((sets,)),
            dma((sets,)),
            dma((STEPS, sets)),
            dma((STEPS, sets)),
            dma((STEPS, sets)),
            dma((STEPS, sets)),
            dma((group,)),
            dma((group,)),
        ],
        compiler_params=pltpu.CompilerParams(collective_id=0, has_side_effects=True),
    )(electric, magnetic, density, design_mask, planes, profiles, waveforms)


def solution(mesh):
    return jax.shard_map(
        functools.partial(shards, mesh.shape["gx"], mesh.shape["gy"]),
        mesh=mesh,
        in_specs=(
            P(None, None, ("cand", "gx"), "gy", None),
            P(None, None, ("cand", "gx"), "gy", None),
            P(("cand", "gx"), "gy", None),
            P(("cand", "gx"), "gy", None),
            P("cand"),
            P(None, ("cand", "gx"), "gy"),
            P(None, "cand"),
        ),
        out_specs=(
            P(None, None, ("cand", "gx"), "gy", None),
            P(None, None, ("cand", "gx"), "gy", None),
            P(("cand", "gx"), "gy", None),
        ),
        check_vma=False,
    )
```

time: 209 us -> 57.1 us (0.27)
  starting transfers between devices: 102 us -> 0 us
  Pallas kernels: 0 us -> 52.8 us
  blocking collectives: 34.8 us -> 0 us
  waiting for transfers between devices: 29.1 us -> 0 us
  other arithmetic: 24.6 us -> 0 us
  local copies, waits for them, and re-layouts: 13.3 us -> 3.32 us
  between operations: 3.08 us -> 0.65 us
    ppermute x44 -> x0, starting transfers between devices: 102 us -> none  [the longest x22 73.8 us: with_halo(): lax.ppermute(lax.slice_in_dim(block, block.shape[dim] - width, None, axis...]
    pallas_call x0 -> x1, Pallas kernels: none -> 52.8 us  [shards(): pl.pallas_call(functools.partial(kernel, count_x, count_y), out_shape=(ja...]
    psum x1 -> x0, blocking collectives: 34.8 us -> none  [shards(): power = lax.psum(local_power, ('gx', 'gy')) / (total_x * total_y)]
    ppermute x44 -> x0, waiting for transfers between devices: 29.1 us -> none  [the longest x22 18.8 us: with_halo(): lax.ppermute(lax.slice_in_dim(block, block.shape[dim] - width, None, axis...]
    mul x23 -> x0, other arithmetic: 13.8 us -> none  [the longest x2 5.12 us: shards(): source_wide * waveforms[0, step]]
    slice x87 -> x0, local copies, waits for them, and re-layouts: 7.33 us -> none  [the longest x16 2.11 us: fwd_z(): field[..., 1:]]
    another operation x24 -> x0, other arithmetic: 5.31 us -> none  [the longest x16 3.79 us: electric_update(): return jnp.stack([new_x, new_y, new_z], 1)]
  transfers between devices with their start and end apart: 44 -> 0, of which waited for: 12 -> 0; matrix products, arithmetic and copies ran while one was open for 10% -> 0% of each run, Pallas kernels for 0% -> 0%
where the time goes in v1:
time: 57.1 us; the launch traced here: 56.8 us
  Pallas kernels  52.8 us (92%)
  local copies, waits for them, and re-layouts  3.32 us (6%)
  between operations  0.65 us (1%)
    pallas_call x1, Pallas kernels, shards(): pl.pallas_call(functools.partial(kernel, count_x, count_y), out_shape=(ja...  52.8 us
    unnamed x7, local copies, waits for them, and re-layouts  3.32 us

profile of v1, /device:TPU:0, one launch (start us, length us, event | category | flops | bytes accessed | tf_op | source)
XLA Modules:
  0.0 56.8 jit_solution(16000985066287286627)
XLA Ops:
  0.6 52.8 %shard_map.94 = (f32[2,3,4,32,128]{4,3,2,1,0:T(8,128)}, f32[2,3,4,32,128]{4,3,2,1,0:T(8,128)}, f32[4,32,128]{2,1,0:T(8,128)}) custom-call(f32[2,3,4,32,128]{4,3,2,1,0:T(8,128)} %electric.1, f32[2,3,4,32,128]{4,3,2,1,0:T(8,128)} %magnetic.1, f32[4,32,128]{2,1,0:T(8,128)} %density.1, s32[4,32,128]{2,1,0:T(8,128)} %mask.1, s32[2]{0:T(128)} %planes.1, ...), custom_call_target="tpu_custom_call" | custom-call | tf_op jit(solution)/shard_map/pallas_call | solution.py:429
  53.5 0.0 copy-start
  53.5 1.8 %copy.13 = f32[2,3,4,32,128]{4,3,2,1,0:T(8,128)} copy(f32[2,3,4,32,128]{4,3,2,1,0:T(8,128)} %get-tuple-element.6) | data formatting | bytes 786432
  55.3 0.0 copy-done
  55.3 0.0 copy-start.1
  55.3 0.7 %copy.14 = f32[2,3,4,32,128]{4,3,2,1,0:T(8,128)} copy(f32[2,3,4,32,128]{4,3,2,1,0:T(8,128)S(1)} %copy-done) | data formatting | bytes 786432
  56.1 0.1 copy-done.1
  56.2 0.6 %copy.15 = f32[4,32,128]{2,1,0:T(8,128)} copy(f32[4,32,128]{2,1,0:T(8,128)S(1)} %copy-done.1) | data formatting | bytes 131072
Async XLA Ops:
  53.5 1.8 %copy-start = (f32[2,3,4,32,128]{4,3,2,1,0:T(8,128)S(1)}, f32[2,3,4,32,128]{4,3,2,1,0:T(8,128)}, u32[]{:S(2)}) copy-start(f32[2,3,4,32,128]{4,3,2,1,0:T(8,128)} %get-tuple-element.7) | copy-start | bytes 1179652
  55.3 0.9 %copy-start.1 = (f32[4,32,128]{2,1,0:T(8,128)S(1)}, f32[4,32,128]{2,1,0:T(8,128)}, u32[]{:S(2)}) copy-start(f32[4,32,128]{2,1,0:T(8,128)} %get-tuple-element.8) | copy-start | bytes 196612

commit v2 on v1

--- a/solution.py
+++ b/solution.py
@@ -35,11 +35,11 @@
     count_y,
     electric,
     magnetic,
-    density,
-    mask,
-    planes,
-    profiles,
-    waves,
+    density_far,
+    mask_far,
+    planes_far,
+    profiles_far,
+    waves_far,
     electric_out,
     magnetic_out,
     gradient_out,
@@ -56,12 +56,15 @@
     power_mine,
     power_all,
     grad,
+    density,
+    mask,
+    planes,
+    profiles,
+    waves,
     load_sem,
     store_sem,
     side_send,
     side_recv,
-    first_send,
-    first_recv,
     up_send,
     up_recv,
     down_send,
@@ -85,34 +88,45 @@
         at = lax.rem(me + j, group)
         return at, {"gx": at // count_y, "gy": lax.rem(at, count_y)}
 
-    barrier = pltpu.get_barrier_semaphore()
-
-    def greet(j, carry):
-        pl.semaphore_signal(barrier, inc=1, device_id=peer(j)[1], device_id_type=MESH)
-        return carry
-
-    lax.fori_loop(1, group, greet, 0)
-
+
+    small = [
+        pltpu.make_async_copy(far, near, load_sem.at[2 + k])
+        for k, (far, near) in enumerate(
+            (
+                (density_far, density),
+                (mask_far, mask),
+                (profiles_far, profiles),
+                (planes_far, planes),
+                (waves_far, waves),
+            )
+        )
+    ]
     loads = [
         pltpu.make_async_copy(electric, elec.at[:, :, :, pl.ds(own, wy), :], load_sem.at[0]),
         pltpu.make_async_copy(
             magnetic, magn.at[:, :, pl.ds(1, wx), pl.ds(own + TILE, wy), :], load_sem.at[1]
         ),
     ]
-    for load in loads:
+    for load in small + loads:
         load.start()
 
     elec[:, :, :, rows:, :] = jnp.zeros((sets, comps, wx, TILE, depth_z), jnp.float32)
     magn[:, :, 1:, :TILE, :] = jnp.zeros((sets, comps, wx, TILE, depth_z), jnp.float32)
 
-    @pl.when(gx == 0)
-    def _():
-        magn[:, 1:, 0, TILE:, :] = jnp.zeros((sets, comps - 1, rows, depth_z), jnp.float32)
+    barrier = pltpu.get_barrier_semaphore()
+
+    def greet(j, carry):
+        pl.semaphore_signal(barrier, inc=1, device_id=peer(j)[1], device_id_type=MESH)
+        return carry
+
+    lax.fori_loop(1, group, greet, 0)
 
     corr[...] = jnp.zeros_like(corr)
     decay, gain = coefficients(depth_z, PMLW)
     gain_half = gain * inv_spacing
     lane = lax.broadcasted_iota(jnp.int32, (1, depth_z), 1)
+    for load in small:
+        load.wait()
     flags = mask[...].astype(jnp.float32)
     inv_eps = 1.0 / (1.0 + contrast * density[...] * flags)
     front[...] = flags * contrast * inv_eps * inv_eps * step_dt
@@ -181,28 +195,23 @@
             device_id_type=MESH,
         )
 
-    def first_copy(s):
-        return pltpu.make_async_remote_copy(
-            src_ref=magn.at[s, pl.ds(1, 2), wx, pl.ds(TILE, rows), :],
-            dst_ref=magn.at[s, pl.ds(1, 2), 0, pl.ds(TILE, rows), :],
-            send_sem=first_send.at[s],
-            recv_sem=first_recv.at[s],
-            device_id=upper,
-            device_id_type=MESH,
-        )
-
-    def send(e, s):
+    def send_high(e, s):
         ex = elec[s, 0, last, :rows, :]
-        send_up[e, s, 0] = (next_z(ex) - ex) * inv_spacing + elec[s, 2, last, :rows, :]
-        send_up[e, s, 1] = (elec[s, 0, last, 1 : rows + 1, :] - ex) * inv_spacing + elec[
-            s, 1, last, :rows, :
-        ]
-        send_down[e, s, 0] = elec[s, 1, 0, :rows, :]
-        send_down[e, s, 1] = elec[s, 2, 0, :rows, :]
+        ey = elec[s, 1, last, :rows, :]
+        ez = elec[s, 2, last, :rows, :]
+        ex_y = elec[s, 0, last, 1 : rows + 1, :]
+        hy = magn[s, 1, wx, TILE:, :]
+        hz = magn[s, 2, wx, TILE:, :]
+        send_up[e, s, 0] = decay * hy - gain_half * (next_z(ex) - ex) - gain * ez
+        send_up[e, s, 1] = decay * hz + gain * ey + gain_half * (ex_y - ex)
 
         @pl.when(gx < count_x - 1)
         def _():
             up_copy(e, s).start()
+
+    def send_low(e, s):
+        send_down[e, s, 0] = elec[s, 1, 0, :rows, :]
+        send_down[e, s, 1] = elec[s, 2, 0, :rows, :]
 
         @pl.when(gx > 0)
         def _():
@@ -255,35 +264,46 @@
         for x in range(1, last):
             electric_at(t, s, x)
 
-    def outer(t, s):
-        @pl.when(gx > 0)
-        def _():
-            up_copy(t, s).wait_recv()
-
+    def outer_high(t, s):
         @pl.when(gx < count_x - 1)
         def _():
             down_copy(t, s).wait_recv()
 
-        inside = jnp.where(gx < count_x - 1, 1, 0)
-        keep = jnp.broadcast_to(inside, (rows, depth_z)) == 1
+        keep = jnp.broadcast_to(jnp.where(gx < count_x - 1, 1, 0), (rows, depth_z)) == 1
         magnetic_at(
             s,
             last,
             jnp.where(keep, from_high[t, s, 0], 0.0),
             jnp.where(keep, from_high[t, s, 1], 0.0),
         )
-        hy = magn[s, 1, 0, TILE:, :]
-        hz = magn[s, 2, 0, TILE:, :]
-        there = jnp.broadcast_to(jnp.where(gx > 0, 1, 0), (rows, depth_z)) == 1
+        electric_at(t, s, last)
+
+    def outer_low(t, s):
+        @pl.when(gx > 0)
+        def _():
+            up_copy(t, s).wait_recv()
+
+        keep = jnp.broadcast_to(jnp.where(gx > 0, 1, 0), (rows, depth_z)) == 1
         magn[s, 1, 0, TILE:, :] = jnp.where(
-            there, decay * hy - gain * (from_low[t, s, 0] - elec[s, 2, 0, :rows, :]), 0.0
+            keep, from_low[t, s, 0] + gain * elec[s, 2, 0, :rows, :], 0.0
         )
         magn[s, 2, 0, TILE:, :] = jnp.where(
-            there, decay * hz - gain * (elec[s, 1, 0, :rows, :] - from_low[t, s, 1]), 0.0
+            keep, from_low[t, s, 1] - gain * elec[s, 1, 0, :rows, :], 0.0
         )
         electric_at(t, s, 0)
-        if last > 0:
-            electric_at(t, s, last)
+
+    def edges(t, order, more):
+        for kind, s in order:
+            if kind:
+                outer_high(t, s)
+                if more:
+                    send_high(t + 1, s)
+            else:
+                outer_low(t, s)
+                if more:
+                    send_low(t + 1, s)
+
+    even = lax.rem(gx, 2) == 0
 
     def correlate():
         for x in range(wx):
@@ -293,29 +313,20 @@
             corr[x] = total
 
     for s in range(sets):
-        send(0, s)
-
-        @pl.when(gx < count_x - 1)
-        def _():
-            first_copy(s).start()
+        send_high(0, s)
+        send_low(0, s)
 
     for s in range(sets):
         inner(0, s)
 
-    for s in range(sets):
-
-        @pl.when(gx > 0)
-        def _():
-            first_copy(s).wait_recv()
-
-        @pl.when(gx < count_x - 1)
-        def _():
-            first_copy(s).wait_send()
-
     def step(t, carry):
-        for s in range(sets):
-            outer(t, s)
-            send(t + 1, s)
+        for parity in range(2):
+
+            @pl.when(even if parity == 0 else jnp.logical_not(even))
+            def _():
+                near = 1 - parity
+                edges(t, ((1 - near, 0), (near, 0), (1 - near, 1), (near, 1)), True)
+
         correlate()
         for s in range(sets):
             inner(t + 1, s)
@@ -346,7 +357,8 @@
             device_id_type=MESH,
         )
 
-    outer(STEPS - 1, 0)
+    outer_low(STEPS - 1, 0)
+    outer_high(STEPS - 1, 0)
     local = jnp.zeros((TILE, depth_z), jnp.float32)
     for c in range(comps):
         for x in range(wx):
@@ -354,7 +366,7 @@
             square = field * field
             for k in range(wy // TILE):
                 local = local + square[k * TILE : (k + 1) * TILE, :]
-    local = jnp.where(lane == planes[1], local, 0.0)
+    local = jnp.where(lane == planes[1], jnp.sum(local, axis=0, keepdims=True), 0.0)
     power_mine[...] = local
     power_all[me] = local
 
@@ -366,7 +378,8 @@
     for copy in give(0):
         copy.start()
 
-    outer(STEPS - 1, 1)
+    outer_low(STEPS - 1, 1)
+    outer_high(STEPS - 1, 1)
     for copy in give(1):
         copy.start()
     correlate()
@@ -381,8 +394,8 @@
     def add(j, total):
         return total + power_all[j]
 
-    total = lax.fori_loop(0, group, add, jnp.zeros((TILE, depth_z), jnp.float32))
-    power = jnp.sum(jnp.sum(total, axis=0, keepdims=True), axis=1, keepdims=True)
+    total = lax.fori_loop(0, group, add, jnp.zeros((1, depth_z), jnp.float32))
+    power = jnp.sum(total, axis=1, keepdims=True)
     power = power / (wx * count_x * wy * count_y)
     scale = 1.0 / (power + small_eps)
     for x in range(wx):
@@ -418,14 +431,12 @@
 
 def shards(count_x, count_y, electric, magnetic, density, design_mask, planes, profiles, waveforms):
     sets, comps, wx, wy, depth_z = electric.shape
-    assert count_y == 2 and STEPS <= TILE
+    assert count_y == 2 and STEPS <= TILE and wx > 1
     rows = wy + TILE
     group = count_x * count_y
     f32 = jnp.float32
     dma = pltpu.SemaphoreType.DMA
     hbm = pl.BlockSpec(memory_space=pl.ANY)
-    vmem = pl.BlockSpec(memory_space=pltpu.VMEM)
-    smem = pl.BlockSpec(memory_space=pltpu.SMEM)
     return pl.pallas_call(
         functools.partial(kernel, count_x, count_y),
         out_shape=(
@@ -433,7 +444,7 @@
             jax.ShapeDtypeStruct(magnetic.shape, f32),
             jax.ShapeDtypeStruct(density.shape, f32),
         ),
-        in_specs=[hbm, hbm, vmem, vmem, smem, vmem, smem],
+        in_specs=[hbm] * 7,
         out_specs=(hbm, hbm, hbm),
         scratch_shapes=[
             pltpu.VMEM((sets, comps, wx, rows + TILE, depth_z), f32),
@@ -446,15 +457,18 @@
             pltpu.VMEM((STEPS, sets, 2, rows, depth_z), f32),
             pltpu.VMEM((STEPS, sets, 2, rows, depth_z), f32),
             pltpu.VMEM((STEPS, sets, 2, rows, depth_z), f32),
-            pltpu.VMEM((TILE, depth_z), f32),
-            pltpu.VMEM((group, TILE, depth_z), f32),
+            pltpu.VMEM((1, depth_z), f32),
+            pltpu.VMEM((group, 1, depth_z), f32),
             pltpu.VMEM((wx, wy, depth_z), f32),
-            dma((2,)),
+            pltpu.VMEM(density.shape, f32),
+            pltpu.VMEM(density.shape, jnp.int32),
+            pltpu.SMEM(planes.shape, jnp.int32),
+            pltpu.VMEM(profiles.shape, f32),
+            pltpu.SMEM(waveforms.shape, f32),
+            dma((7,)),
             dma((2, sets)),
             dma((4,)),
             dma((4,)),
-            dma((sets,)),
-            dma((sets,)),
             dma((STEPS, sets)),
             dma((STEPS, sets)),
             dma((STEPS, sets)),

time: 57.1 us -> 51.5 us (0.902)
  Pallas kernels: 52.8 us -> 47.4 us
    pallas_call x1, Pallas kernels: 52.8 us -> 47.4 us  [shards(): pl.pallas_call(functools.partial(kernel, count_x, count_y), out_shape=(ja...]
where the time goes in v2:
time: 51.5 us; the launch traced here: 51.3 us
  Pallas kernels  47.4 us (92%)
  local copies, waits for them, and re-layouts  3.32 us (6%)
  between operations  0.65 us (1%)
    pallas_call x1, Pallas kernels, shards(): pl.pallas_call(functools.partial(kernel, count_x, count_y), out_shape=(ja...  47.4 us
    unnamed x7, local copies, waits for them, and re-layouts  3.32 us

profile of v2, /device:TPU:0, one launch (start us, length us, event | category | flops | bytes accessed | tf_op | source)
XLA Modules:
  0.0 51.3 jit_solution(16501975314539877745)
XLA Ops:
  0.6 47.4 %shard_map.94 = (f32[2,3,4,32,128]{4,3,2,1,0:T(8,128)}, f32[2,3,4,32,128]{4,3,2,1,0:T(8,128)}, f32[4,32,128]{2,1,0:T(8,128)}) custom-call(f32[2,3,4,32,128]{4,3,2,1,0:T(8,128)} %electric.1, f32[2,3,4,32,128]{4,3,2,1,0:T(8,128)} %magnetic.1, f32[4,32,128]{2,1,0:T(8,128)} %density_far.1, s32[4,32,128]{2,1,0:T(8,128)} %mask_far.1, s32[2]{0:T(128)} %planes_far.1, ...), custom_call_target="tpu_custom_call" | custom-call | tf_op jit(solution)/shard_map/pallas_call | solution.py:440
  48.0 0.0 copy-start
  48.0 1.8 %copy.13 = f32[2,3,4,32,128]{4,3,2,1,0:T(8,128)} copy(f32[2,3,4,32,128]{4,3,2,1,0:T(8,128)} %get-tuple-element.6) | data formatting | bytes 786432
  49.8 0.0 copy-done
  49.8 0.0 copy-start.1
  49.8 0.7 %copy.14 = f32[2,3,4,32,128]{4,3,2,1,0:T(8,128)} copy(f32[2,3,4,32,128]{4,3,2,1,0:T(8,128)S(1)} %copy-done) | data formatting | bytes 786432
  50.6 0.1 copy-done.1
  50.7 0.6 %copy.15 = f32[4,32,128]{2,1,0:T(8,128)} copy(f32[4,32,128]{2,1,0:T(8,128)S(1)} %copy-done.1) | data formatting | bytes 131072
Async XLA Ops:
  48.0 1.8 %copy-start = (f32[2,3,4,32,128]{4,3,2,1,0:T(8,128)S(1)}, f32[2,3,4,32,128]{4,3,2,1,0:T(8,128)}, u32[]{:S(2)}) copy-start(f32[2,3,4,32,128]{4,3,2,1,0:T(8,128)} %get-tuple-element.7) | copy-start | bytes 1179652
  49.8 0.9 %copy-start.1 = (f32[4,32,128]{2,1,0:T(8,128)S(1)}, f32[4,32,128]{2,1,0:T(8,128)}, u32[]{:S(2)}) copy-start(f32[4,32,128]{2,1,0:T(8,128)} %get-tuple-element.8) | copy-start | bytes 196612

commit v3 on v2

--- a/solution.py
+++ b/solution.py
@@ -53,6 +53,10 @@
     send_down,
     from_low,
     from_high,
+    send_side,
+    from_side,
+    send_slant,
+    from_slant,
     power_mine,
     power_all,
     grad,
@@ -63,8 +67,10 @@
     waves,
     load_sem,
     store_sem,
-    side_send,
+    side_sent,
     side_recv,
+    slant_sent,
+    slant_recv,
     up_send,
     up_recv,
     down_send,
@@ -73,7 +79,8 @@
     power_recv,
 ):
     sets, comps, wx, wy, depth_z = electric.shape
-    rows = wy + TILE
+    rows = wy
+    edge = wy - 1
     last = wx - 1
     gx = lax.axis_index("gx")
     gy = lax.axis_index("gy")
@@ -82,7 +89,7 @@
     other = {"gy": 1 - gy}
     upper = {"gx": lax.rem(gx + 1, count_x)}
     lower = {"gx": lax.rem(gx + count_x - 1, count_x)}
-    own = pl.multiple_of(gy * TILE, TILE)
+    own = 0
 
     def peer(j):
         at = lax.rem(me + j, group)
@@ -145,35 +152,78 @@
         load.wait()
     pl.semaphore_wait(barrier, group - 1)
 
-    take = pl.multiple_of((1 - gy) * (wy - TILE) + gy * TILE, TILE)
-    put = pl.multiple_of(gy * wy, TILE)
-    spots = [
-        (elec, (slice(None),) * 3, 0),
-        (magn, (slice(None), slice(None), pl.ds(1, wx)), TILE),
-        (scaled, (slice(None),), 0),
-        (source, (slice(None),) * 2, 0),
-    ]
-    sides = [
-        pltpu.make_async_remote_copy(
-            src_ref=ref.at[(*lead, pl.ds(take + base, TILE), slice(None))],
-            dst_ref=ref.at[(*lead, pl.ds(put + base, TILE), slice(None))],
-            send_sem=side_send.at[k],
-            recv_sem=side_recv.at[k],
+    def next_z(f):
+        return jnp.where(lane < depth_z - 1, pltpu.roll(f, depth_z - 1, 1), 0.0)
+
+    def previous_z(f):
+        return jnp.where(lane > 0, pltpu.roll(f, 1, 1), 0.0)
+
+    def side_copy(e, s):
+        return pltpu.make_async_remote_copy(
+            src_ref=send_side.at[e, s],
+            dst_ref=from_side.at[e, s],
+            send_sem=side_sent.at[e, s],
+            recv_sem=side_recv.at[e, s],
             device_id=other,
             device_id_type=MESH,
         )
-        for k, (ref, lead, base) in enumerate(spots)
-    ]
-    for side in sides:
-        side.start()
-    for side in sides:
-        side.wait()
-
-    def next_z(f):
-        return jnp.where(lane < depth_z - 1, pltpu.roll(f, depth_z - 1, 1), 0.0)
-
-    def previous_z(f):
-        return jnp.where(lane > 0, pltpu.roll(f, 1, 1), 0.0)
+
+    def slant_copy(e, s):
+        return pltpu.make_async_remote_copy(
+            src_ref=send_slant.at[e, s],
+            dst_ref=from_slant.at[e, s],
+            send_sem=slant_sent.at[e, s],
+            recv_sem=slant_recv.at[e, s],
+            device_id={
+                "gx": lax.rem(gx + count_x - 1 + 2 * gy, count_x),
+                "gy": 1 - gy,
+            },
+            device_id_type=MESH,
+        )
+
+    def send_beside(e, s):
+        @pl.when(gy == 0)
+        def _():
+            for x in range(wx):
+                ex = elec[s, 0, x, edge : edge + 1, :]
+                ey = elec[s, 1, x, edge : edge + 1, :]
+                ez = elec[s, 2, x, edge : edge + 1, :]
+                hx = magn[s, 0, x + 1, TILE + edge : TILE + wy, :]
+                hz = magn[s, 2, x + 1, TILE + edge : TILE + wy, :]
+                slope = ey if x == last else ey - elec[s, 1, x + 1, edge : edge + 1, :]
+                send_side[e, s, x : x + 1, :] = decay * hx + gain_half * (ez + (next_z(ey) - ey))
+                send_side[e, s, wx + x : wx + x + 1, :] = (
+                    decay * hz + gain * slope - gain_half * ex
+                )
+
+        @pl.when(gy == 1)
+        def _():
+            for x in range(wx):
+                send_side[e, s, x : x + 1, :] = elec[s, 0, x, 0:1, :]
+                send_side[e, s, wx + x : wx + x + 1, :] = elec[s, 2, x, 0:1, :]
+
+        side_copy(e, s).start()
+
+    def take_beside(t, s):
+        side_copy(t, s).wait_recv()
+
+        @pl.when(gy == 0)
+        def _():
+            for x in range(wx):
+                elec[s, 0, x, wy : wy + 1, :] = from_side[t, s, x : x + 1, :]
+                elec[s, 2, x, wy : wy + 1, :] = from_side[t, s, wx + x : wx + x + 1, :]
+
+        @pl.when(gy == 1)
+        def _():
+            for x in range(wx):
+                magn[s, 0, x + 1, TILE - 1 : TILE, :] = (
+                    from_side[t, s, x : x + 1, :] - gain_half * elec[s, 2, x, 0:1, :]
+                )
+                magn[s, 2, x + 1, TILE - 1 : TILE, :] = (
+                    from_side[t, s, wx + x : wx + x + 1, :] + gain_half * elec[s, 0, x, 0:1, :]
+                )
+
+    below_edge = lax.broadcasted_iota(jnp.int32, (rows, depth_z), 0) < edge
 
     def up_copy(e, s):
         return pltpu.make_async_remote_copy(
@@ -199,7 +249,7 @@
         ex = elec[s, 0, last, :rows, :]
         ey = elec[s, 1, last, :rows, :]
         ez = elec[s, 2, last, :rows, :]
-        ex_y = elec[s, 0, last, 1 : rows + 1, :]
+        ex_y = jnp.where(below_edge, elec[s, 0, last, 1 : rows + 1, :], 0.0)
         hy = magn[s, 1, wx, TILE:, :]
         hz = magn[s, 2, wx, TILE:, :]
         send_up[e, s, 0] = decay * hy - gain_half * (next_z(ex) - ex) - gain * ez
@@ -209,6 +259,11 @@
         def _():
             up_copy(e, s).start()
 
+        @pl.when((gx < count_x - 1) & (gy == 1))
+        def _():
+            send_slant[e, s] = elec[s, 0, last, 0:1, :]
+            slant_copy(e, s).start()
+
     def send_low(e, s):
         send_down[e, s, 0] = elec[s, 1, 0, :rows, :]
         send_down[e, s, 1] = elec[s, 2, 0, :rows, :]
@@ -216,6 +271,11 @@
         @pl.when(gx > 0)
         def _():
             down_copy(e, s).start()
+
+        @pl.when((gx > 0) & (gy == 0))
+        def _():
+            send_slant[e, s] = elec[s, 1, 0, edge : edge + 1, :]
+            slant_copy(e, s).start()
 
     def magnetic_at(s, x, ey_next, ez_next):
         ex = elec[s, 0, x, :rows, :]
@@ -259,6 +319,7 @@
         )
 
     def inner(t, s):
+        take_beside(t, s)
         for x in range(last):
             magnetic_at(s, x, elec[s, 1, x + 1, :rows, :], elec[s, 2, x + 1, :rows, :])
         for x in range(1, last):
@@ -276,6 +337,14 @@
             jnp.where(keep, from_high[t, s, 0], 0.0),
             jnp.where(keep, from_high[t, s, 1], 0.0),
         )
+
+        @pl.when((gx < count_x - 1) & (gy == 1))
+        def _():
+            slant_copy(t, s).wait_recv()
+            magn[s, 2, wx, TILE - 1 : TILE, :] = (
+                magn[s, 2, wx, TILE - 1 : TILE, :] - gain * from_slant[t, s]
+            )
+
         electric_at(t, s, last)
 
     def outer_low(t, s):
@@ -290,10 +359,18 @@
         magn[s, 2, 0, TILE:, :] = jnp.where(
             keep, from_low[t, s, 1] - gain * elec[s, 1, 0, :rows, :], 0.0
         )
+
+        @pl.when((gx > 0) & (gy == 0))
+        def _():
+            slant_copy(t, s).wait_recv()
+            magn[s, 2, 0, TILE + edge :, :] = (
+                magn[s, 2, 0, TILE + edge :, :] + gain_half * from_slant[t, s]
+            )
+
         electric_at(t, s, 0)
 
     def edges(t, order, more):
-        for kind, s in order:
+        for at, (kind, s) in enumerate(order):
             if kind:
                 outer_high(t, s)
                 if more:
@@ -302,6 +379,8 @@
                 outer_low(t, s)
                 if more:
                     send_low(t + 1, s)
+            if more and at % 2 == 1:
+                send_beside(t + 1, s)
 
     even = lax.rem(gx, 2) == 0
 
@@ -315,6 +394,7 @@
     for s in range(sets):
         send_high(0, s)
         send_low(0, s)
+        send_beside(0, s)
 
     for s in range(sets):
         inner(0, s)
@@ -411,6 +491,11 @@
 
     def drain(e, carry):
         for s in range(sets):
+            side_copy(e, s).wait_send()
+
+            @pl.when(((gx > 0) & (gy == 0)) | ((gx < count_x - 1) & (gy == 1)))
+            def _():
+                slant_copy(e, s).wait_send()
 
             @pl.when(gx < count_x - 1)
             def _():
@@ -431,8 +516,8 @@
 
 def shards(count_x, count_y, electric, magnetic, density, design_mask, planes, profiles, waveforms):
     sets, comps, wx, wy, depth_z = electric.shape
-    assert count_y == 2 and STEPS <= TILE and wx > 1
-    rows = wy + TILE
+    assert count_y == 2 and wx > 1
+    rows = wy
     group = count_x * count_y
     f32 = jnp.float32
     dma = pltpu.SemaphoreType.DMA
@@ -457,6 +542,10 @@
             pltpu.VMEM((STEPS, sets, 2, rows, depth_z), f32),
             pltpu.VMEM((STEPS, sets, 2, rows, depth_z), f32),
             pltpu.VMEM((STEPS, sets, 2, rows, depth_z), f32),
+            pltpu.VMEM((STEPS, sets, 2 * wx, depth_z), f32),
+            pltpu.VMEM((STEPS, sets, 2 * wx, depth_z), f32),
+            pltpu.VMEM((STEPS, sets, 1, depth_z), f32),
+            pltpu.VMEM((STEPS, sets, 1, depth_z), f32),
             pltpu.VMEM((1, depth_z), f32),
             pltpu.VMEM((group, 1, depth_z), f32),
             pltpu.VMEM((wx, wy, depth_z), f32),
@@ -467,8 +556,10 @@
             pltpu.SMEM(waveforms.shape, f32),
             dma((7,)),
             dma((2, sets)),
-            dma((4,)),
-            dma((4,)),
+            dma((STEPS, sets)),
+            dma((STEPS, sets)),
+            dma((STEPS, sets)),
+            dma((STEPS, sets)),
             dma((STEPS, sets)),
             dma((STEPS, sets)),
             dma((STEPS, sets)),

time: 51.5 us -> 45.9 us (0.89)
  Pallas kernels: 47.4 us -> 41.7 us
    pallas_call x1, Pallas kernels: 47.4 us -> 41.7 us  [shards(): pl.pallas_call(functools.partial(kernel, count_x, count_y), out_shape=(ja...]
where the time goes in v3:
time: 45.9 us; the launch traced here: 45.6 us
  Pallas kernels  41.7 us (91%)
  local copies, waits for them, and re-layouts  3.32 us (7%)
  between operations  0.65 us (1%)
    pallas_call x1, Pallas kernels, shards(): pl.pallas_call(functools.partial(kernel, count_x, count_y), out_shape=(ja...  41.7 us
    unnamed x7, local copies, waits for them, and re-layouts  3.32 us

profile of v3, /device:TPU:0, one launch (start us, length us, event | category | flops | bytes accessed | tf_op | source)
XLA Modules:
  0.0 45.6 jit_solution(15559456289127298503)
XLA Ops:
  0.6 41.7 %shard_map.94 = (f32[2,3,4,32,128]{4,3,2,1,0:T(8,128)}, f32[2,3,4,32,128]{4,3,2,1,0:T(8,128)}, f32[4,32,128]{2,1,0:T(8,128)}) custom-call(f32[2,3,4,32,128]{4,3,2,1,0:T(8,128)} %electric.1, f32[2,3,4,32,128]{4,3,2,1,0:T(8,128)} %magnetic.1, f32[4,32,128]{2,1,0:T(8,128)} %density_far.1, s32[4,32,128]{2,1,0:T(8,128)} %mask_far.1, s32[2]{0:T(128)} %planes_far.1, ...), custom_call_target="tpu_custom_call" | custom-call | tf_op jit(solution)/shard_map/pallas_call | solution.py:525
  42.3 0.0 copy-start
  42.3 1.8 %copy.13 = f32[2,3,4,32,128]{4,3,2,1,0:T(8,128)} copy(f32[2,3,4,32,128]{4,3,2,1,0:T(8,128)} %get-tuple-element.6) | data formatting | bytes 786432
  44.2 0.0 copy-done
  44.2 0.0 copy-start.1
  44.2 0.7 %copy.14 = f32[2,3,4,32,128]{4,3,2,1,0:T(8,128)} copy(f32[2,3,4,32,128]{4,3,2,1,0:T(8,128)S(1)} %copy-done) | data formatting | bytes 786432
  44.9 0.1 copy-done.1
  45.0 0.6 %copy.15 = f32[4,32,128]{2,1,0:T(8,128)} copy(f32[4,32,128]{2,1,0:T(8,128)S(1)} %copy-done.1) | data formatting | bytes 131072
Async XLA Ops:
  42.3 1.8 %copy-start = (f32[2,3,4,32,128]{4,3,2,1,0:T(8,128)S(1)}, f32[2,3,4,32,128]{4,3,2,1,0:T(8,128)}, u32[]{:S(2)}) copy-start(f32[2,3,4,32,128]{4,3,2,1,0:T(8,128)} %get-tuple-element.7) | copy-start | bytes 1179652
  44.2 0.9 %copy-start.1 = (f32[4,32,128]{2,1,0:T(8,128)S(1)}, f32[4,32,128]{2,1,0:T(8,128)}, u32[]{:S(2)}) copy-start(f32[4,32,128]{2,1,0:T(8,128)} %get-tuple-element.8) | copy-start | bytes 196612

commit v4 on v3

--- a/solution.py
+++ b/solution.py
@@ -255,27 +255,27 @@
         send_up[e, s, 0] = decay * hy - gain_half * (next_z(ex) - ex) - gain * ez
         send_up[e, s, 1] = decay * hz + gain * ey + gain_half * (ex_y - ex)
 
-        @pl.when(gx < count_x - 1)
-        def _():
-            up_copy(e, s).start()
-
         @pl.when((gx < count_x - 1) & (gy == 1))
         def _():
             send_slant[e, s] = elec[s, 0, last, 0:1, :]
             slant_copy(e, s).start()
+
+        @pl.when(gx < count_x - 1)
+        def _():
+            up_copy(e, s).start()
 
     def send_low(e, s):
         send_down[e, s, 0] = elec[s, 1, 0, :rows, :]
         send_down[e, s, 1] = elec[s, 2, 0, :rows, :]
 
-        @pl.when(gx > 0)
-        def _():
-            down_copy(e, s).start()
-
         @pl.when((gx > 0) & (gy == 0))
         def _():
             send_slant[e, s] = elec[s, 1, 0, edge : edge + 1, :]
             slant_copy(e, s).start()
+
+        @pl.when(gx > 0)
+        def _():
+            down_copy(e, s).start()
 
     def magnetic_at(s, x, ey_next, ez_next):
         ex = elec[s, 0, x, :rows, :]
@@ -514,6 +514,19 @@
     last_copy.wait()
 
 
+def write_out(electric, magnetic, gradient, electric_out, magnetic_out, gradient_out, sems):
+    copies = [
+        pltpu.make_async_copy(near, far, sems.at[k])
+        for k, (near, far) in enumerate(
+            ((electric, electric_out), (magnetic, magnetic_out), (gradient, gradient_out))
+        )
+    ]
+    for copy in copies:
+        copy.start()
+    for copy in copies:
+        copy.wait()
+
+
 def shards(count_x, count_y, electric, magnetic, density, design_mask, planes, profiles, waveforms):
     sets, comps, wx, wy, depth_z = electric.shape
     assert count_y == 2 and wx > 1
@@ -522,7 +535,7 @@
     f32 = jnp.float32
     dma = pltpu.SemaphoreType.DMA
     hbm = pl.BlockSpec(memory_space=pl.ANY)
-    return pl.pallas_call(
+    results = pl.pallas_call(
         functools.partial(kernel, count_x, count_y),
         out_shape=(
             jax.ShapeDtypeStruct(electric.shape, f32),
@@ -569,6 +582,13 @@
         ],
         compiler_params=pltpu.CompilerParams(collective_id=0, has_side_effects=True),
     )(electric, magnetic, density, design_mask, planes, profiles, waveforms)
+    return pl.pallas_call(
+        write_out,
+        out_shape=tuple(jax.ShapeDtypeStruct(r.shape, f32) for r in results),
+        in_specs=[pl.BlockSpec(memory_space=pltpu.VMEM)] * 3,
+        out_specs=(hbm, hbm, hbm),
+        scratch_shapes=[dma((3,))],
+    )(*results)
 
 
 def solution(mesh):

time: 45.9 us -> 43.7 us (0.952)
  local copies, waits for them, and re-layouts: 3.32 us -> 0 us
  Pallas kernels: 41.7 us -> 42.9 us
    unnamed x7 -> x0, local copies, waits for them, and re-layouts: 3.32 us -> none
    pallas_call x0 -> x1, Pallas kernels: none -> 2.03 us  [shards(): pl.pallas_call(write_out, out_shape=tuple((jax.ShapeDtypeStruct(r.shape,...]
    pallas_call x1, Pallas kernels: 41.7 us -> 40.9 us  [shards(): pl.pallas_call(functools.partial(kernel, count_x, count_y), out_shape=(ja...]
where the time goes in v4:
time: 43.7 us; the launch traced here: 43.6 us
  Pallas kernels  42.9 us (98%)
  between operations  0.64 us (1%)
    pallas_call x1, Pallas kernels, shards(): pl.pallas_call(functools.partial(kernel, count_x, count_y), out_shape=(ja...  40.9 us
    pallas_call x1, Pallas kernels, shards(): pl.pallas_call(write_out, out_shape=tuple((jax.ShapeDtypeStruct(r.shape,...  2.03 us

profile of v4, /device:TPU:0, one launch (start us, length us, event | category | flops | bytes accessed | tf_op | source)
XLA Modules:
  0.0 43.6 jit_solution(13757395871019026438)
XLA Ops:
  0.6 40.9 %shard_map.94 = (f32[2,3,4,32,128]{4,3,2,1,0:T(8,128)}, f32[2,3,4,32,128]{4,3,2,1,0:T(8,128)}, f32[4,32,128]{2,1,0:T(8,128)}) custom-call(f32[2,3,4,32,128]{4,3,2,1,0:T(8,128)} %electric.1, f32[2,3,4,32,128]{4,3,2,1,0:T(8,128)} %magnetic.1, f32[4,32,128]{2,1,0:T(8,128)} %density_far.1, s32[4,32,128]{2,1,0:T(8,128)} %mask_far.1, s32[2]{0:T(128)} %planes_far.1, ...), custom_call_target="tpu_custom_call" | custom-call | tf_op jit(solution)/shard_map/pallas_call | solution.py:538
  41.5 2.0 %shard_map.95 = (f32[2,3,4,32,128]{4,3,2,1,0:T(8,128)}, f32[2,3,4,32,128]{4,3,2,1,0:T(8,128)}, f32[4,32,128]{2,1,0:T(8,128)}) custom-call(f32[2,3,4,32,128]{4,3,2,1,0:T(8,128)} %get-tuple-element.6.electric, f32[2,3,4,32,128]{4,3,2,1,0:T(8,128)} %get-tuple-element.7.magnetic, f32[4,32,128]{2,1,0:T(8,128)} %get-tuple-element.8.gradient), custom_call_target="tpu_custom_call" | custom-call | tf_op jit(solution)/shard_map/pallas_call | solution.py:585
